TPU v7x, 256 devices: a whole 4x4x8 slice. The times are simulated.
256 devices in a mesh: dp: 32 (over x, y, core), tensor: 8 (over z).
Axes of the slice: x: 4, y: 4, z: 8, core: 2. Of those that a mesh axis runs over, the one named last changes fastest.
Arguments:
- img_hidden: bfloat16 [32768, 4304], P('dp', 'tensor'), may hold values from -0.25 to 0.25
- img_down: bfloat16 [4304, 1152], P('tensor'), may hold values from -0.09375 to 0.09375
- img_pooled: bfloat16 [32768, 1152], P(('dp', 'tensor')), may hold values from -0.25 to 0.25
- txt_hidden: bfloat16 [32768, 1152], P('dp', 'tensor'), may hold values from -0.25 to 0.25
- txt_proj: bfloat16 [1152, 1152], P('tensor'), may hold values from -0.1875 to 0.1875
- log_temp: float32 [1], replicated, may hold values from 1 to 2
- bias: float32 [1], replicated, may hold values from -4 to -1
- match: int32 [32768], P(('dp', 'tensor')), may hold values from 0 to 32767
- window_index: int32 [1], replicated, may hold values from 0 to 15
Outputs:
- img_grad: float32 [32768, 1152], P(('dp', 'tensor'))
- txt_grad: float32 [32768, 1152], P(('dp', 'tensor'))
- row_loss: float32 [32768], P(('dp', 'tensor'))
All inputs are finite; a program needn't handle non-finite values.
Results may differ from a plain program's by a relative error of at most 0.0039.
Values may be sent and summed in bfloat16 or wider, within the bound.
A program may use at most 64 MiB of HBM per device.

v0:
```python
import jax
import jax.numpy as jnp
from jax import lax
from jax.sharding import PartitionSpec as P

STEPS = 16


def shifted(shard, axis, by):
    devices = lax.axis_size(axis)
    return lax.ppermute(shard, axis, [(i, (i + by) % devices) for i in range(devices)])


def unit_rows(emb):
    length = jnp.sqrt(jnp.sum(emb * emb, axis=1, keepdims=True) + 1e-06)
    return (emb / length, length)


def pair_tile(image_low, text_block, owner, match, scale, shift_value):
    cosine = lax.dot_general(
        image_low, text_block, (((1,), (1,)), ((), ())), preferred_element_type=jnp.float32
    )
    text_index = owner * text_block.shape[0] + lax.iota(jnp.int32, text_block.shape[0])
    positive = match[:, None] == text_index[None, :]
    logit = scale * cosine + shift_value
    pair_loss = jnp.sum(
        jnp.where(positive, jax.nn.softplus(-logit), jax.nn.softplus(logit)), axis=1
    )
    coef = ((jax.nn.sigmoid(logit) - positive.astype(jnp.float32)) * scale).astype(jnp.bfloat16)
    image_part = jnp.dot(coef, text_block, preferred_element_type=jnp.float32)
    text_part = lax.dot_general(
        coef, image_low, (((0,), (0,)), ((), ())), preferred_element_type=jnp.float32
    )
    return (pair_loss, image_part, text_part)


def offset_blocks(blocks, window):
    windows = lax.axis_size(("dp", "tensor")) // STEPS
    for level in range((windows - 1).bit_length()):
        moved = shifted(blocks, ("dp", "tensor"), STEPS << level)
        blocks = jnp.where(window >> level & 1 == 1, moved, blocks)
    return blocks


def return_home(text_sum, fixed_steps, window):
    text_sum = shifted(text_sum, ("dp", "tensor"), -fixed_steps)
    windows = lax.axis_size(("dp", "tensor")) // STEPS
    for level in range((windows - 1).bit_length()):
        moved = shifted(text_sum, ("dp", "tensor"), -(STEPS << level))
        text_sum = jnp.where(window >> level & 1 == 1, moved, text_sum)
    return text_sum


def body(
    img_hidden, img_down, img_pooled, txt_hidden, txt_proj, log_temp, bias, match, window_index
):
    width = img_pooled.shape[1]
    summed = lax.psum_scatter(
        jnp.concatenate(
            [
                jnp.dot(img_hidden, img_down, preferred_element_type=jnp.float32),
                jnp.dot(txt_hidden, txt_proj, preferred_element_type=jnp.float32),
            ],
            axis=1,
        ),
        "tensor",
        scatter_dimension=0,
        tiled=True,
    )
    img_emb = summed[:, :width] + img_pooled.astype(jnp.float32)
    txt_emb = summed[:, width:]
    img_unit, img_len = unit_rows(img_emb)
    txt_unit, txt_len = unit_rows(txt_emb)
    image_low = img_unit.astype(jnp.bfloat16)
    text_low = txt_unit.astype(jnp.bfloat16)
    scale = jnp.exp(log_temp[0])
    shift_value = bias[0]
    window = window_index[0]
    start_step = window * STEPS
    position = lax.axis_index(("dp", "tensor"))
    devices = lax.axis_size(("dp", "tensor"))
    half_steps = STEPS // 2
    late_copy = shifted(text_low, ("dp", "tensor"), STEPS - 1)
    stacked = offset_blocks(jnp.stack([text_low, late_copy]), window)
    early_block = stacked[0]
    late_block = stacked[1]
    early_owner = (position - start_step) % devices
    late_owner = (position - start_step - (STEPS - 1)) % devices
    early_loss, early_image, early_sum = pair_tile(
        image_low, early_block, early_owner, match, scale, shift_value
    )
    late_loss, late_image, late_sum = pair_tile(
        image_low, late_block, late_owner, match, scale, shift_value
    )

    def two_turn(turn, carry):
        early_now, late_now, early_acc, late_acc, image_now, loss_now = carry
        early_now = shifted(early_now, ("dp", "tensor"), 1)
        late_now = shifted(late_now, ("dp", "tensor"), -1)
        early_acc = shifted(early_acc, ("dp", "tensor"), 1)
        late_acc = shifted(late_acc, ("dp", "tensor"), -1)
        owner_early = (position - start_step - turn) % devices
        owner_late = (position - start_step - (STEPS - 1) + turn) % devices
        loss_one, image_one, text_one = pair_tile(
            image_low, early_now, owner_early, match, scale, shift_value
        )
        loss_two, image_two, text_two = pair_tile(
            image_low, late_now, owner_late, match, scale, shift_value
        )
        return (
            early_now,
            late_now,
            early_acc + text_one,
            late_acc + text_two,
            image_now + image_one + image_two,
            loss_now + loss_one + loss_two,
        )

    carried = lax.fori_loop(
        1,
        half_steps,
        two_turn,
        (
            early_block,
            late_block,
            early_sum,
            late_sum,
            early_image + late_image,
            early_loss + late_loss,
        ),
    )
    early_sum = carried[2]
    late_sum = carried[3]
    image_dunit = carried[4]
    row_loss = carried[5]
    late_moved = shifted(late_sum, ("dp", "tensor"), -1)
    text_dunit = return_home(early_sum + late_moved, half_steps - 1, window)
    img_grad = (
        image_dunit - img_unit * jnp.sum(img_unit * image_dunit, axis=1, keepdims=True)
    ) / img_len
    txt_grad = (
        text_dunit - txt_unit * jnp.sum(txt_unit * text_dunit, axis=1, keepdims=True)
    ) / txt_len
    return (img_grad, txt_grad, row_loss)


def solution(mesh):
    in_specs = (
        P("dp", "tensor"),
        P("tensor", None),
        P(("dp", "tensor"), None),
        P("dp", "tensor"),
        P("tensor", None),
        P(),
        P(),
        P(("dp", "tensor")),
        P(),
    )
    out_specs = (P(("dp", "tensor"), None), P(("dp", "tensor"), None), P(("dp", "tensor")))
    return jax.shard_map(body, mesh=mesh, in_specs=in_specs, out_specs=out_specs, check_vma=False)
```

profile of v0, /device:TPU:1, one launch (start us, length us, event | category | flops | bytes accessed | tf_op | source)
XLA Modules:
  0.0 487.4 jit_solution(13462369484042464486)
XLA Ops:
  8.5 5.7 %fusion.44 = f32[1024,1152]{1,0:T(8,128)} fusion(bf16[1024,538]{0,1:T(8,128)(2,1)} %param.11, bf16[538,1152]{1,0:T(8,128)(2,1)S(1)} %copy-done), kind=kOutput, calls=%fused_computation.95 | convolution fusion | flops 1269301248 | bytes 7059968 | tf_op jit(solution)/shard_map/dot_general | solution.py:61
  15.0 6.7 %pad_maximum_fusion = f32[1024,2304]{1,0:T(8,128)} fusion(f32[1024,1152]{1,0:T(8,128)S(1)} %fusion.45, f32[1024,1152]{1,0:T(8,128)} %fusion.44), kind=kLoop, calls=%fused_computation.36 | loop fusion | flops 2359296 | bytes 18874368 | tf_op jit(solution)/shard_map/concatenate | solution.py:59
  21.8 108.7 %reduce-scatter.2.cloned.1.call-done = f32[128,2304]{1,0:T(8,128)} async-done(((f32[1024,2304]{1,0:T(8,128)}), f32[128,2304]{1,0:T(8,128)}) %reduce-scatter.2.cloned.1.call-update) | async-done | bytes 1179664 | tf_op jit(solution)/shard_map/reduce_scatter | solution.py:58
  132.3 2.7 collective-permute-start.4
  135.0 9.4 %collective-permute-done.4 = bf16[128,1152]{1,0:T(8,128)(2,1)S(1)} collective-permute-done((bf16[128,1152]{1,0:T(8,128)(2,1)S(1)}, bf16[128,1152]{1,0:T(8,128)(2,1)S(1)}, u32[]{:S(2)}, u32[]{:S(2)}) %collective-permute-start.4) | collective-permute-done | bytes 294944 | tf_op jit(solution)/shard_map/ppermute | solution.py:11
  145.2 15.9 %collective-permute-done.5 = bf16[2,128,1152]{2,1,0:T(8,128)(2,1)S(1)} collective-permute-done((bf16[2,128,1152]{2,1,0:T(8,128)(2,1)S(1)}, bf16[2,128,1152]{2,1,0:T(8,128)(2,1)S(1)}, u32[]{:S(2)}, u32[]{:S(2)}) %collective-permute-start.5) | collective-permute-done | bytes 589856 | tf_op jit(solution)/shard_map/ppermute | solution.py:11
  161.3 16.0 %collective-permute-done.6 = bf16[2,128,1152]{2,1,0:T(8,128)(2,1)S(1)} collective-permute-done((bf16[2,128,1152]{2,1,0:T(8,128)(2,1)S(1)}, bf16[2,128,1152]{2,1,0:T(8,128)(2,1)S(1)}, u32[]{:S(2)}, u32[]{:S(2)}) %collective-permute-start.6) | collective-permute-done | bytes 589856 | tf_op jit(solution)/shard_map/ppermute | solution.py:11
  177.6 11.9 %collective-permute-done.7 = bf16[2,128,1152]{2,1,0:T(8,128)(2,1)S(1)} collective-permute-done((bf16[2,128,1152]{2,1,0:T(8,128)(2,1)S(1)}, bf16[2,128,1152]{2,1,0:T(8,128)(2,1)S(1)}, u32[]{:S(2)}, u32[]{:S(2)}) %collective-permute-start.7) | collective-permute-done | bytes 589856 | tf_op jit(solution)/shard_map/ppermute | solution.py:11
  191.2 8.9 %collective-permute-done.8 = bf16[2,128,1152]{2,1,0:T(8,128)(2,1)S(1)} collective-permute-done((bf16[2,128,1152]{2,1,0:T(8,128)(2,1)S(1)}, bf16[2,128,1152]{2,1,0:T(8,128)(2,1)S(1)}, u32[]{:S(2)}, u32[]{:S(2)}) %collective-permute-start.8) | collective-permute-done | bytes 589856 | tf_op jit(solution)/shard_map/ppermute | solution.py:11
  204.5 186.0 %while.25 = (s32[]{:T(128)}, bf16[128,1152]{1,0:T(8,128)(2,1)}, bf16[128,1152]{1,0:T(8,128)(2,1)}, f32[128,1152]{1,0:T(8,128)}, f32[128,1152]{1,0:T(8,128)}, /*i...) while((s32[]{:T(128)}, bf16[128,1152]{1,0:T(8,128)(2,1)}, ...), condition=%wide.region_8.9_spmd, body=%wide.region_5.8_spmd.sunk | while | flops 228196640 | bytes 15804535 | solution.py:119
  206.4 3.1 collective-permute-start.2
  209.6 9.8 %collective-permute-start.3 = (f32[128,1152]{1,0:T(8,128)}, f32[128,1152]{1,0:T(8,128)S(1)}, u32[]{:S(2)}, u32[]{:S(2)}) collective-permute-start(f32[128,1152]{1,0:T(8,128)} %get-tuple-element.483), channel_id=1, source_target_pairs={{0,255},{1,0},{2,1},{3,2},{4,3},{5,4},{6,5},{7,6},{8,7},{9,8},{10,... | collective-permute-start | bytes 1769480 | tf_op jit(solution)/shard_map/while/body/eval_jaxpr/ppermute | solution.py:11
  220.6 5.2 %collective-permute-done = bf16[128,1152]{1,0:T(8,128)(2,1)S(1)} collective-permute-done((bf16[128,1152]{1,0:T(8,128)(2,1)}, bf16[128,1152]{1,0:T(8,128)(2,1)S(1)}, u32[]{:S(2)}, u32[]{:S(2)}) %collective-permute-start) | collective-permute-done | bytes 294944 | tf_op jit(solution)/shard_map/while/body/eval_jaxpr/ppermute | solution.py:11
  228.6 3.6 collective-permute-done.2
  232.2 2.2 convolution_add_fusion.6
  236.9 3.6 collective-permute-start.3
  242.5 5.9 %collective-permute-done = bf16[128,1152]{1,0:T(8,128)(2,1)S(1)} collective-permute-done((bf16[128,1152]{1,0:T(8,128)(2,1)}, bf16[128,1152]{1,0:T(8,128)(2,1)S(1)}, u32[]{:S(2)}, u32[]{:S(2)}) %collective-permute-start) | collective-permute-done | bytes 294944 | tf_op jit(solution)/shard_map/while/body/eval_jaxpr/ppermute | solution.py:11
  251.2 6.3 %collective-permute-done.2 = f32[128,1152]{1,0:T(8,128)} collective-permute-done((f32[128,1152]{1,0:T(8,128)}, f32[128,1152]{1,0:T(8,128)}, u32[]{:S(2)}, u32[]{:S(2)}) %collective-permute-start.2) | collective-permute-done | bytes 589856 | tf_op jit(solution)/shard_map/while/body/eval_jaxpr/ppermute | solution.py:11
  257.5 2.2 convolution_add_fusion.6
  262.3 2.9 collective-permute-start.3
  267.8 4.1 collective-permute-done
  274.7 7.4 %collective-permute-done.2 = f32[128,1152]{1,0:T(8,128)} collective-permute-done((f32[128,1152]{1,0:T(8,128)}, f32[128,1152]{1,0:T(8,128)}, u32[]{:S(2)}, u32[]{:S(2)}) %collective-permute-start.2) | collective-permute-done | bytes 589856 | tf_op jit(solution)/shard_map/while/body/eval_jaxpr/ppermute | solution.py:11
  282.1 2.2 convolution_add_fusion.6
  286.8 3.0 collective-permute-start.3
  289.8 2.3 collective-permute-done.1
  293.3 4.1 collective-permute-done
  300.2 7.4 %collective-permute-done.2 = f32[128,1152]{1,0:T(8,128)} collective-permute-done((f32[128,1152]{1,0:T(8,128)}, f32[128,1152]{1,0:T(8,128)}, u32[]{:S(2)}, u32[]{:S(2)}) %collective-permute-start.2) | collective-permute-done | bytes 589856 | tf_op jit(solution)/shard_map/while/body/eval_jaxpr/ppermute | solution.py:11
  307.7 2.2 convolution_add_fusion.6
  312.4 2.9 collective-permute-start.3
  315.4 3.3 collective-permute-done.1
  324.5 9.6 %collective-permute-done.2 = f32[128,1152]{1,0:T(8,128)} collective-permute-done((f32[128,1152]{1,0:T(8,128)}, f32[128,1152]{1,0:T(8,128)}, u32[]{:S(2)}, u32[]{:S(2)}) %collective-permute-start.2) | collective-permute-done | bytes 589856 | tf_op jit(solution)/shard_map/while/body/eval_jaxpr/ppermute | solution.py:11
  334.1 2.2 convolution_add_fusion.6
  338.9 2.9 collective-permute-start.3
  341.8 3.5 collective-permute-done.1
  350.9 10.2 %collective-permute-done.2 = f32[128,1152]{1,0:T(8,128)} collective-permute-done((f32[128,1152]{1,0:T(8,128)}, f32[128,1152]{1,0:T(8,128)}, u32[]{:S(2)}, u32[]{:S(2)}) %collective-permute-start.2) | collective-permute-done | bytes 589856 | tf_op jit(solution)/shard_map/while/body/eval_jaxpr/ppermute | solution.py:11
  361.1 2.2 convolution_add_fusion.6
  365.9 2.9 collective-permute-start.3
  368.8 2.7 collective-permute-done.1
  372.8 2.0 collective-permute-done
  377.6 9.6 %collective-permute-done.2 = f32[128,1152]{1,0:T(8,128)} collective-permute-done((f32[128,1152]{1,0:T(8,128)}, f32[128,1152]{1,0:T(8,128)}, u32[]{:S(2)}, u32[]{:S(2)}) %collective-permute-start.2) | collective-permute-done | bytes 589856 | tf_op jit(solution)/shard_map/while/body/eval_jaxpr/ppermute | solution.py:11
  387.3 2.2 convolution_add_fusion.6
  390.5 14.8 %collective-permute-done.9 = f32[128,1152]{1,0:T(8,128)S(1)} collective-permute-done((f32[128,1152]{1,0:T(8,128)}, f32[128,1152]{1,0:T(8,128)S(1)}, u32[]{:S(2)}, u32[]{:S(2)}) %collective-permute-start.9) | collective-permute-done | bytes 589856 | tf_op jit(solution)/shard_map/ppermute | solution.py:11
  407.0 16.0 %collective-permute-done.10 = f32[128,1152]{1,0:T(8,128)S(1)} collective-permute-done((f32[128,1152]{1,0:T(8,128)S(1)}, f32[128,1152]{1,0:T(8,128)S(1)}, u32[]{:S(2)}, u32[]{:S(2)}) %collective-permute-start.10) | collective-permute-done | bytes 589856 | tf_op jit(solution)/shard_map/ppermute | solution.py:11
  423.0 13.6 %collective-permute-done.11 = f32[128,1152]{1,0:T(8,128)S(1)} collective-permute-done((f32[128,1152]{1,0:T(8,128)S(1)}, f32[128,1152]{1,0:T(8,128)S(1)}, u32[]{:S(2)}, u32[]{:S(2)}) %collective-permute-start.11) | collective-permute-done | bytes 589856 | tf_op jit(solution)/shard_map/ppermute | solution.py:11
  436.8 14.2 %collective-permute-done.12 = f32[128,1152]{1,0:T(8,128)S(1)} collective-permute-done((f32[128,1152]{1,0:T(8,128)S(1)}, f32[128,1152]{1,0:T(8,128)S(1)}, u32[]{:S(2)}, u32[]{:S(2)}) %collective-permute-start.12) | collective-permute-done | bytes 589856 | tf_op jit(solution)/shard_map/ppermute | solution.py:11
  451.2 13.6 %collective-permute-done.13 = f32[128,1152]{1,0:T(8,128)S(1)} collective-permute-done((f32[128,1152]{1,0:T(8,128)S(1)}, f32[128,1152]{1,0:T(8,128)S(1)}, u32[]{:S(2)}, u32[]{:S(2)}) %collective-permute-start.13) | collective-permute-done | bytes 589856 | tf_op jit(solution)/shard_map/ppermute | solution.py:11
  464.9 2.7 collective-permute-start.14
  467.6 11.3 %collective-permute-done.14 = f32[128,1152]{1,0:T(8,128)S(1)} collective-permute-done((f32[128,1152]{1,0:T(8,128)S(1)}, f32[128,1152]{1,0:T(8,128)S(1)}, u32[]{:S(2)}, u32[]{:S(2)}) %collective-permute-start.14) | collective-permute-done | bytes 589856 | tf_op jit(solution)/shard_map/ppermute | solution.py:11
  (148 shorter events, 65.0 us)
Async XLA Ops:
  7.2 6.9 %copy-start.7 = (bf16[1024,144]{0,1:T(8,128)(2,1)S(1)}, bf16[1024,144]{0,1:T(8,128)(2,1)}, u32[]{:S(2)}) copy-start(bf16[1024,144]{0,1:T(8,128)(2,1)} %param.14) | copy-start | bytes 884740
  7.2 6.9 %copy-start.5 = (bf16[144,1152]{1,0:T(8,128)(2,1)S(1)}, bf16[144,1152]{1,0:T(8,128)(2,1)}, u32[]{:S(2)}) copy-start(bf16[144,1152]{1,0:T(8,128)(2,1)} %param.15) | copy-start | bytes 995332
  7.2 123.3 %reduce-scatter.2.cloned.1.call-start = ((), (), s32[]{:S(2)}) async-start(), calls=%async_computation.1 | async-start | bytes 10616832 | tf_op jit(solution)/shard_map/reduce_scatter | solution.py:58
  21.7 108.7 %copy-start.3 = (bf16[128,1152]{1,0:T(8,128)(2,1)S(1)}, bf16[128,1152]{1,0:T(8,128)(2,1)}, u32[]{:S(2)}) copy-start(bf16[128,1152]{1,0:T(8,128)(2,1)} %param.13) | copy-start | bytes 884740
  130.5 1.6 copy-start.1
  132.3 12.1 %collective-permute-start.4 = (bf16[128,1152]{1,0:T(8,128)(2,1)S(1)}, bf16[128,1152]{1,0:T(8,128)(2,1)S(1)}, u32[]{:S(2)}, u32[]{:S(2)}) collective-permute-start(bf16[128,1152]{1,0:T(8,128)(2,1)S(1)} %get-tuple-element.364), channel_id=1, source_target_pairs={{0,15},{1,16},{2,17},{3,18},{4,19},{5,20},{6,21},{7,22},{8,23},{9,... | collective-permute-start | bytes 884744 | tf_op jit(solution)/shard_map/ppermute | solution.py:11
  144.5 16.7 %collective-permute-start.5 = (bf16[2,128,1152]{2,1,0:T(8,128)(2,1)S(1)}, bf16[2,128,1152]{2,1,0:T(8,128)(2,1)S(1)}, u32[]{:S(2)}, u32[]{:S(2)}) collective-permute-start(bf16[2,128,1152]{2,1,0:T(8,128)(2,1)S(1)} %pad_maximum_fusion.1), channel_id=1, source_target_pairs={{0,16},{1,17},{2,18},{3,19},{4,20},{5,21},{6,22},{7,23},{8,24},{9,... | collective-permute-start | bytes 1769480 | tf_op jit(solution)/shard_map/ppermute | solution.py:11
  161.3 16.1 %collective-permute-start.6 = (bf16[2,128,1152]{2,1,0:T(8,128)(2,1)S(1)}, bf16[2,128,1152]{2,1,0:T(8,128)(2,1)S(1)}, u32[]{:S(2)}, u32[]{:S(2)}) collective-permute-start(bf16[2,128,1152]{2,1,0:T(8,128)(2,1)S(1)} %broadcast_select_fusion), channel_id=1, source_target_pairs={{0,32},{1,33},{2,34},{3,35},{4,36},{5,37},{6,38},{7,39},{8,40},{9,... | collective-permute-start | bytes 1769480 | tf_op jit(solution)/shard_map/ppermute | solution.py:11
  177.5 12.0 %collective-permute-start.7 = (bf16[2,128,1152]{2,1,0:T(8,128)(2,1)S(1)}, bf16[2,128,1152]{2,1,0:T(8,128)(2,1)S(1)}, u32[]{:S(2)}, u32[]{:S(2)}) collective-permute-start(bf16[2,128,1152]{2,1,0:T(8,128)(2,1)S(1)} %broadcast_select_fusion.1), channel_id=1, source_target_pairs={{0,64},{1,65},{2,66},{3,67},{4,68},{5,69},{6,70},{7,71},{8,72},{9,... | collective-permute-start | bytes 1769480 | tf_op jit(solution)/shard_map/ppermute | solution.py:11
  189.5 10.6 %collective-permute-start.8 = (bf16[2,128,1152]{2,1,0:T(8,128)(2,1)S(1)}, bf16[2,128,1152]{2,1,0:T(8,128)(2,1)S(1)}, u32[]{:S(2)}, u32[]{:S(2)}) collective-permute-start(bf16[2,128,1152]{2,1,0:T(8,128)(2,1)S(1)} %broadcast_select_fusion.2), channel_id=1, source_target_pairs={{0,128},{1,129},{2,130},{3,131},{4,132},{5,133},{6,134},{7,135},{8... | collective-permute-start | bytes 1769480 | tf_op jit(solution)/shard_map/ppermute | solution.py:11
  189.8 10.6 %copy-start.6 = (s32[128]{0:T(128)S(1)}, s32[128]{0:T(128)}, u32[]{:S(2)}) copy-start(s32[128]{0:T(128)} %param.18) | copy-start | bytes 1540
  204.6 14.8 %collective-permute-start.1 = (bf16[128,1152]{1,0:T(8,128)(2,1)}, bf16[128,1152]{1,0:T(8,128)(2,1)S(1)}, u32[]{:S(2)}, u32[]{:S(2)}) collective-permute-start(bf16[128,1152]{1,0:T(8,128)(2,1)} %get-tuple-element.481), channel_id=1, source_target_pairs={{0,255},{1,0},{2,1},{3,2},{4,3},{5,4},{6,5},{7,6},{8,7},{9,8},{10,... | collective-permute-start | bytes 884744 | tf_op jit(solution)/shard_map/while/body/eval_jaxpr/ppermute | solution.py:11
  206.4 19.3 %collective-permute-start = (bf16[128,1152]{1,0:T(8,128)(2,1)}, bf16[128,1152]{1,0:T(8,128)(2,1)S(1)}, u32[]{:S(2)}, u32[]{:S(2)}) collective-permute-start(bf16[128,1152]{1,0:T(8,128)(2,1)} %get-tuple-element.480), channel_id=1, source_target_pairs={{0,1},{1,2},{2,3},{3,4},{4,5},{5,6},{6,7},{7,8},{8,9},{9,10},{10,1... | collective-permute-start | bytes 884744 | tf_op jit(solution)/shard_map/while/body/eval_jaxpr/ppermute | solution.py:11
  206.4 25.7 %collective-permute-start.2 = (f32[128,1152]{1,0:T(8,128)}, f32[128,1152]{1,0:T(8,128)}, u32[]{:S(2)}, u32[]{:S(2)}) collective-permute-start(f32[128,1152]{1,0:T(8,128)} %get-tuple-element.482), channel_id=1, source_target_pairs={{0,1},{1,2},{2,3},{3,4},{4,5},{5,6},{6,7},{7,8},{8,9},{9,10},{10,1... | collective-permute-start | bytes 1769480 | tf_op jit(solution)/shard_map/while/body/eval_jaxpr/ppermute | solution.py:11
  209.6 24.8 %collective-permute-start.3 = (f32[128,1152]{1,0:T(8,128)}, f32[128,1152]{1,0:T(8,128)S(1)}, u32[]{:S(2)}, u32[]{:S(2)}) collective-permute-start(f32[128,1152]{1,0:T(8,128)} %get-tuple-element.483), channel_id=1, source_target_pairs={{0,255},{1,0},{2,1},{3,2},{4,3},{5,4},{6,5},{7,6},{8,7},{9,8},{10,... | collective-permute-start | bytes 1769480 | tf_op jit(solution)/shard_map/while/body/eval_jaxpr/ppermute | solution.py:11
  235.5 5.8 %collective-permute-start.1 = (bf16[128,1152]{1,0:T(8,128)(2,1)}, bf16[128,1152]{1,0:T(8,128)(2,1)S(1)}, u32[]{:S(2)}, u32[]{:S(2)}) collective-permute-start(bf16[128,1152]{1,0:T(8,128)(2,1)} %get-tuple-element.481), channel_id=1, source_target_pairs={{0,255},{1,0},{2,1},{3,2},{4,3},{5,4},{6,5},{7,6},{8,7},{9,8},{10,... | collective-permute-start | bytes 884744 | tf_op jit(solution)/shard_map/while/body/eval_jaxpr/ppermute | solution.py:11
  236.0 12.4 %collective-permute-start = (bf16[128,1152]{1,0:T(8,128)(2,1)}, bf16[128,1152]{1,0:T(8,128)(2,1)S(1)}, u32[]{:S(2)}, u32[]{:S(2)}) collective-permute-start(bf16[128,1152]{1,0:T(8,128)(2,1)} %get-tuple-element.480), channel_id=1, source_target_pairs={{0,1},{1,2},{2,3},{3,4},{4,5},{5,6},{6,7},{7,8},{8,9},{9,10},{10,1... | collective-permute-start | bytes 884744 | tf_op jit(solution)/shard_map/while/body/eval_jaxpr/ppermute | solution.py:11
  236.9 20.6 %collective-permute-start.2 = (f32[128,1152]{1,0:T(8,128)}, f32[128,1152]{1,0:T(8,128)}, u32[]{:S(2)}, u32[]{:S(2)}) collective-permute-start(f32[128,1152]{1,0:T(8,128)} %get-tuple-element.482), channel_id=1, source_target_pairs={{0,1},{1,2},{2,3},{3,4},{4,5},{5,6},{6,7},{7,8},{8,9},{9,10},{10,1... | collective-permute-start | bytes 1769480 | tf_op jit(solution)/shard_map/while/body/eval_jaxpr/ppermute | solution.py:11
  236.9 22.7 %collective-permute-start.3 = (f32[128,1152]{1,0:T(8,128)}, f32[128,1152]{1,0:T(8,128)S(1)}, u32[]{:S(2)}, u32[]{:S(2)}) collective-permute-start(f32[128,1152]{1,0:T(8,128)} %get-tuple-element.483), channel_id=1, source_target_pairs={{0,255},{1,0},{2,1},{3,2},{4,3},{5,4},{6,5},{7,6},{8,7},{9,8},{10,... | collective-permute-start | bytes 1769480 | tf_op jit(solution)/shard_map/while/body/eval_jaxpr/ppermute | solution.py:11
  260.8 5.8 %collective-permute-start.1 = (bf16[128,1152]{1,0:T(8,128)(2,1)}, bf16[128,1152]{1,0:T(8,128)(2,1)S(1)}, u32[]{:S(2)}, u32[]{:S(2)}) collective-permute-start(bf16[128,1152]{1,0:T(8,128)(2,1)} %get-tuple-element.481), channel_id=1, source_target_pairs={{0,255},{1,0},{2,1},{3,2},{4,3},{5,4},{6,5},{7,6},{8,7},{9,8},{10,... | collective-permute-start | bytes 884744 | tf_op jit(solution)/shard_map/while/body/eval_jaxpr/ppermute | solution.py:11
  260.8 11.1 %collective-permute-start = (bf16[128,1152]{1,0:T(8,128)(2,1)}, bf16[128,1152]{1,0:T(8,128)(2,1)S(1)}, u32[]{:S(2)}, u32[]{:S(2)}) collective-permute-start(bf16[128,1152]{1,0:T(8,128)(2,1)} %get-tuple-element.480), channel_id=1, source_target_pairs={{0,1},{1,2},{2,3},{3,4},{4,5},{5,6},{6,7},{7,8},{8,9},{9,10},{10,1... | collective-permute-start | bytes 884744 | tf_op jit(solution)/shard_map/while/body/eval_jaxpr/ppermute | solution.py:11
  262.2 19.8 %collective-permute-start.2 = (f32[128,1152]{1,0:T(8,128)}, f32[128,1152]{1,0:T(8,128)}, u32[]{:S(2)}, u32[]{:S(2)}) collective-permute-start(f32[128,1152]{1,0:T(8,128)} %get-tuple-element.482), channel_id=1, source_target_pairs={{0,1},{1,2},{2,3},{3,4},{4,5},{5,6},{6,7},{7,8},{8,9},{9,10},{10,1... | collective-permute-start | bytes 1769480 | tf_op jit(solution)/shard_map/while/body/eval_jaxpr/ppermute | solution.py:11
  262.3 22.0 %collective-permute-start.3 = (f32[128,1152]{1,0:T(8,128)}, f32[128,1152]{1,0:T(8,128)S(1)}, u32[]{:S(2)}, u32[]{:S(2)}) collective-permute-start(f32[128,1152]{1,0:T(8,128)} %get-tuple-element.483), channel_id=1, source_target_pairs={{0,255},{1,0},{2,1},{3,2},{4,3},{5,4},{6,5},{7,6},{8,7},{9,8},{10,... | collective-permute-start | bytes 1769480 | tf_op jit(solution)/shard_map/while/body/eval_jaxpr/ppermute | solution.py:11
  285.4 6.7 %collective-permute-start.1 = (bf16[128,1152]{1,0:T(8,128)(2,1)}, bf16[128,1152]{1,0:T(8,128)(2,1)S(1)}, u32[]{:S(2)}, u32[]{:S(2)}) collective-permute-start(bf16[128,1152]{1,0:T(8,128)(2,1)} %get-tuple-element.481), channel_id=1, source_target_pairs={{0,255},{1,0},{2,1},{3,2},{4,3},{5,4},{6,5},{7,6},{8,7},{9,8},{10,... | collective-permute-start | bytes 884744 | tf_op jit(solution)/shard_map/while/body/eval_jaxpr/ppermute | solution.py:11
  286.5 10.9 %collective-permute-start = (bf16[128,1152]{1,0:T(8,128)(2,1)}, bf16[128,1152]{1,0:T(8,128)(2,1)S(1)}, u32[]{:S(2)}, u32[]{:S(2)}) collective-permute-start(bf16[128,1152]{1,0:T(8,128)(2,1)} %get-tuple-element.480), channel_id=1, source_target_pairs={{0,1},{1,2},{2,3},{3,4},{4,5},{5,6},{6,7},{7,8},{8,9},{9,10},{10,1... | collective-permute-start | bytes 884744 | tf_op jit(solution)/shard_map/while/body/eval_jaxpr/ppermute | solution.py:11
  286.8 20.9 %collective-permute-start.2 = (f32[128,1152]{1,0:T(8,128)}, f32[128,1152]{1,0:T(8,128)}, u32[]{:S(2)}, u32[]{:S(2)}) collective-permute-start(f32[128,1152]{1,0:T(8,128)} %get-tuple-element.482), channel_id=1, source_target_pairs={{0,1},{1,2},{2,3},{3,4},{4,5},{5,6},{6,7},{7,8},{8,9},{9,10},{10,1... | collective-permute-start | bytes 1769480 | tf_op jit(solution)/shard_map/while/body/eval_jaxpr/ppermute | solution.py:11
  286.8 23.0 %collective-permute-start.3 = (f32[128,1152]{1,0:T(8,128)}, f32[128,1152]{1,0:T(8,128)S(1)}, u32[]{:S(2)}, u32[]{:S(2)}) collective-permute-start(f32[128,1152]{1,0:T(8,128)} %get-tuple-element.483), channel_id=1, source_target_pairs={{0,255},{1,0},{2,1},{3,2},{4,3},{5,4},{6,5},{7,6},{8,7},{9,8},{10,... | collective-permute-start | bytes 1769480 | tf_op jit(solution)/shard_map/while/body/eval_jaxpr/ppermute | solution.py:11
  310.9 7.7 %collective-permute-start.1 = (bf16[128,1152]{1,0:T(8,128)(2,1)}, bf16[128,1152]{1,0:T(8,128)(2,1)S(1)}, u32[]{:S(2)}, u32[]{:S(2)}) collective-permute-start(bf16[128,1152]{1,0:T(8,128)(2,1)} %get-tuple-element.481), channel_id=1, source_target_pairs={{0,255},{1,0},{2,1},{3,2},{4,3},{5,4},{6,5},{7,6},{8,7},{9,8},{10,... | collective-permute-start | bytes 884744 | tf_op jit(solution)/shard_map/while/body/eval_jaxpr/ppermute | solution.py:11
  310.9 10.7 %collective-permute-start = (bf16[128,1152]{1,0:T(8,128)(2,1)}, bf16[128,1152]{1,0:T(8,128)(2,1)S(1)}, u32[]{:S(2)}, u32[]{:S(2)}) collective-permute-start(bf16[128,1152]{1,0:T(8,128)(2,1)} %get-tuple-element.480), channel_id=1, source_target_pairs={{0,1},{1,2},{2,3},{3,4},{4,5},{5,6},{6,7},{7,8},{8,9},{9,10},{10,1... | collective-permute-start | bytes 884744 | tf_op jit(solution)/shard_map/while/body/eval_jaxpr/ppermute | solution.py:11
  312.4 21.7 %collective-permute-start.2 = (f32[128,1152]{1,0:T(8,128)}, f32[128,1152]{1,0:T(8,128)}, u32[]{:S(2)}, u32[]{:S(2)}) collective-permute-start(f32[128,1152]{1,0:T(8,128)} %get-tuple-element.482), channel_id=1, source_target_pairs={{0,1},{1,2},{2,3},{3,4},{4,5},{5,6},{6,7},{7,8},{8,9},{9,10},{10,1... | collective-permute-start | bytes 1769480 | tf_op jit(solution)/shard_map/while/body/eval_jaxpr/ppermute | solution.py:11
  312.4 23.9 %collective-permute-start.3 = (f32[128,1152]{1,0:T(8,128)}, f32[128,1152]{1,0:T(8,128)S(1)}, u32[]{:S(2)}, u32[]{:S(2)}) collective-permute-start(f32[128,1152]{1,0:T(8,128)} %get-tuple-element.483), channel_id=1, source_target_pairs={{0,255},{1,0},{2,1},{3,2},{4,3},{5,4},{6,5},{7,6},{8,7},{9,8},{10,... | collective-permute-start | bytes 1769480 | tf_op jit(solution)/shard_map/while/body/eval_jaxpr/ppermute | solution.py:11
  337.4 7.9 %collective-permute-start.1 = (bf16[128,1152]{1,0:T(8,128)(2,1)}, bf16[128,1152]{1,0:T(8,128)(2,1)S(1)}, u32[]{:S(2)}, u32[]{:S(2)}) collective-permute-start(bf16[128,1152]{1,0:T(8,128)(2,1)} %get-tuple-element.481), channel_id=1, source_target_pairs={{0,255},{1,0},{2,1},{3,2},{4,3},{5,4},{6,5},{7,6},{8,7},{9,8},{10,... | collective-permute-start | bytes 884744 | tf_op jit(solution)/shard_map/while/body/eval_jaxpr/ppermute | solution.py:11
  337.4 10.7 %collective-permute-start = (bf16[128,1152]{1,0:T(8,128)(2,1)}, bf16[128,1152]{1,0:T(8,128)(2,1)S(1)}, u32[]{:S(2)}, u32[]{:S(2)}) collective-permute-start(bf16[128,1152]{1,0:T(8,128)(2,1)} %get-tuple-element.480), channel_id=1, source_target_pairs={{0,1},{1,2},{2,3},{3,4},{4,5},{5,6},{6,7},{7,8},{8,9},{9,10},{10,1... | collective-permute-start | bytes 884744 | tf_op jit(solution)/shard_map/while/body/eval_jaxpr/ppermute | solution.py:11
  338.9 22.3 %collective-permute-start.2 = (f32[128,1152]{1,0:T(8,128)}, f32[128,1152]{1,0:T(8,128)}, u32[]{:S(2)}, u32[]{:S(2)}) collective-permute-start(f32[128,1152]{1,0:T(8,128)} %get-tuple-element.482), channel_id=1, source_target_pairs={{0,1},{1,2},{2,3},{3,4},{4,5},{5,6},{6,7},{7,8},{8,9},{9,10},{10,1... | collective-permute-start | bytes 1769480 | tf_op jit(solution)/shard_map/while/body/eval_jaxpr/ppermute | solution.py:11
  338.9 24.4 %collective-permute-start.3 = (f32[128,1152]{1,0:T(8,128)}, f32[128,1152]{1,0:T(8,128)S(1)}, u32[]{:S(2)}, u32[]{:S(2)}) collective-permute-start(f32[128,1152]{1,0:T(8,128)} %get-tuple-element.483), channel_id=1, source_target_pairs={{0,255},{1,0},{2,1},{3,2},{4,3},{5,4},{6,5},{7,6},{8,7},{9,8},{10,... | collective-permute-start | bytes 1769480 | tf_op jit(solution)/shard_map/while/body/eval_jaxpr/ppermute | solution.py:11
  364.4 7.2 %collective-permute-start.1 = (bf16[128,1152]{1,0:T(8,128)(2,1)}, bf16[128,1152]{1,0:T(8,128)(2,1)S(1)}, u32[]{:S(2)}, u32[]{:S(2)}) collective-permute-start(bf16[128,1152]{1,0:T(8,128)(2,1)} %get-tuple-element.481), channel_id=1, source_target_pairs={{0,255},{1,0},{2,1},{3,2},{4,3},{5,4},{6,5},{7,6},{8,7},{9,8},{10,... | collective-permute-start | bytes 884744 | tf_op jit(solution)/shard_map/while/body/eval_jaxpr/ppermute | solution.py:11
  364.4 10.4 %collective-permute-start = (bf16[128,1152]{1,0:T(8,128)(2,1)}, bf16[128,1152]{1,0:T(8,128)(2,1)S(1)}, u32[]{:S(2)}, u32[]{:S(2)}) collective-permute-start(bf16[128,1152]{1,0:T(8,128)(2,1)} %get-tuple-element.480), channel_id=1, source_target_pairs={{0,1},{1,2},{2,3},{3,4},{4,5},{5,6},{6,7},{7,8},{8,9},{9,10},{10,1... | collective-permute-start | bytes 884744 | tf_op jit(solution)/shard_map/while/body/eval_jaxpr/ppermute | solution.py:11
  365.9 21.4 %collective-permute-start.2 = (f32[128,1152]{1,0:T(8,128)}, f32[128,1152]{1,0:T(8,128)}, u32[]{:S(2)}, u32[]{:S(2)}) collective-permute-start(f32[128,1152]{1,0:T(8,128)} %get-tuple-element.482), channel_id=1, source_target_pairs={{0,1},{1,2},{2,3},{3,4},{4,5},{5,6},{6,7},{7,8},{8,9},{9,10},{10,1... | collective-permute-start | bytes 1769480 | tf_op jit(solution)/shard_map/while/body/eval_jaxpr/ppermute | solution.py:11
  365.9 23.5 %collective-permute-start.3 = (f32[128,1152]{1,0:T(8,128)}, f32[128,1152]{1,0:T(8,128)S(1)}, u32[]{:S(2)}, u32[]{:S(2)}) collective-permute-start(f32[128,1152]{1,0:T(8,128)} %get-tuple-element.483), channel_id=1, source_target_pairs={{0,255},{1,0},{2,1},{3,2},{4,3},{5,4},{6,5},{7,6},{8,7},{9,8},{10,... | collective-permute-start | bytes 1769480 | tf_op jit(solution)/shard_map/while/body/eval_jaxpr/ppermute | solution.py:11
  390.5 46.2 %copy-start.8 = (f32[128]{0:T(128)}, f32[128]{0:T(128)S(1)}, u32[]{:S(2)}) copy-start(f32[128]{0:T(128)S(1)} %get-tuple-element.319) | copy-start | bytes 1540
  390.5 14.8 %collective-permute-start.9 = (f32[128,1152]{1,0:T(8,128)}, f32[128,1152]{1,0:T(8,128)S(1)}, u32[]{:S(2)}, u32[]{:S(2)}) collective-permute-start(f32[128,1152]{1,0:T(8,128)} %get-tuple-element.322), channel_id=1, source_target_pairs={{0,255},{1,0},{2,1},{3,2},{4,3},{5,4},{6,5},{7,6},{8,7},{9,8},{10,... | collective-permute-start | bytes 1769480 | tf_op jit(solution)/shard_map/ppermute | solution.py:11
  406.5 16.5 %collective-permute-start.10 = (f32[128,1152]{1,0:T(8,128)S(1)}, f32[128,1152]{1,0:T(8,128)S(1)}, u32[]{:S(2)}, u32[]{:S(2)}) collective-permute-start(f32[128,1152]{1,0:T(8,128)S(1)} %add.355), channel_id=1, source_target_pairs={{0,249},{1,250},{2,251},{3,252},{4,253},{5,254},{6,255},{7,0},{8,1... | collective-permute-start | bytes 1769480 | tf_op jit(solution)/shard_map/ppermute | solution.py:11
  423.0 13.6 %collective-permute-start.11 = (f32[128,1152]{1,0:T(8,128)S(1)}, f32[128,1152]{1,0:T(8,128)S(1)}, u32[]{:S(2)}, u32[]{:S(2)}) collective-permute-start(f32[128,1152]{1,0:T(8,128)S(1)} %collective-permute-done.10), channel_id=1, source_target_pairs={{0,240},{1,241},{2,242},{3,243},{4,244},{5,245},{6,246},{7,247},{8... | collective-permute-start | bytes 1769480 | tf_op jit(solution)/shard_map/ppermute | solution.py:11
  436.7 14.3 %collective-permute-start.12 = (f32[128,1152]{1,0:T(8,128)S(1)}, f32[128,1152]{1,0:T(8,128)S(1)}, u32[]{:S(2)}, u32[]{:S(2)}) collective-permute-start(f32[128,1152]{1,0:T(8,128)S(1)} %broadcast_select_fusion.4), channel_id=1, source_target_pairs={{0,224},{1,225},{2,226},{3,227},{4,228},{5,229},{6,230},{7,231},{8... | collective-permute-start | bytes 1769480 | tf_op jit(solution)/shard_map/ppermute | solution.py:11
  451.1 27.8 %copy-start.2 = (f32[128,2304]{1,0:T(8,128)S(1)}, f32[128,2304]{1,0:T(8,128)}, u32[]{:S(2)}) copy-start(f32[128,2304]{1,0:T(8,128)} %reduce-scatter.2.cloned.1.call-done) | copy-start | bytes 3538948
  451.1 27.8 %copy-start.4 = (bf16[128,1152]{1,0:T(8,128)(2,1)S(1)}, bf16[128,1152]{1,0:T(8,128)(2,1)}, u32[]{:S(2)}) copy-start(bf16[128,1152]{1,0:T(8,128)(2,1)} %param.13) | copy-start | bytes 884740
  451.1 13.7 %collective-permute-start.13 = (f32[128,1152]{1,0:T(8,128)S(1)}, f32[128,1152]{1,0:T(8,128)S(1)}, u32[]{:S(2)}, u32[]{:S(2)}) collective-permute-start(f32[128,1152]{1,0:T(8,128)S(1)} %broadcast_select_fusion.5), channel_id=1, source_target_pairs={{0,192},{1,193},{2,194},{3,195},{4,196},{5,197},{6,198},{7,199},{8... | collective-permute-start | bytes 1769480 | tf_op jit(solution)/shard_map/ppermute | solution.py:11
  464.9 14.0 %collective-permute-start.14 = (f32[128,1152]{1,0:T(8,128)S(1)}, f32[128,1152]{1,0:T(8,128)S(1)}, u32[]{:S(2)}, u32[]{:S(2)}) collective-permute-start(f32[128,1152]{1,0:T(8,128)S(1)} %broadcast_select_fusion.6), channel_id=1, source_target_pairs={{0,128},{1,129},{2,130},{3,131},{4,132},{5,133},{6,134},{7,135},{8... | collective-permute-start | bytes 1769480 | tf_op jit(solution)/shard_map/ppermute | solution.py:11
  (1 other events, 1.3 us)
Sparse Core Ops, SparseCore 0:
  21.9 108.5 reduce-scatter.1
where the time goes:
time: 493 us; the launch traced here: 487 us
  waiting for transfers between devices  347 us (70%)
  matrix products  50.9 us (10%)
  starting transfers between devices  48.7 us (10%)
  between operations  16.3 us (3%)
  local copies, waits for them, and re-layouts  12.2 us (2%)
  other arithmetic  12 us (2%)
    ppermute x39, waiting for transfers between devices, shifted(): lax.ppermute(shard, axis, [(i, (i + by) % devices) for i in range(devices)])  238 us
    reduce_scatter x1, waiting for transfers between devices, body(): lax.psum_scatter(jnp.concatenate([jnp.dot(img_hidden, img_down, preferred...  109 us
    ppermute x39, starting transfers between devices, shifted(): lax.ppermute(shard, axis, [(i, (i + by) % devices) for i in range(devices)])  48.6 us
    dot_general x16, matrix products, pair_tile(): lax.dot_general(coef, image_low, (((0,), (0,)), ((), ())), preferred_elem...  25 us
    dot_general x16, matrix products, pair_tile(): lax.dot_general(image_low, text_block, (((1,), (1,)), ((), ())), preferre...  13.8 us
    while x14, local copies, waits for them, and re-layouts  10 us
  transfers between devices with their start and end apart: 40, of which 32 were waited for; matrix products, arithmetic and copies ran while one was open for 9% of the time, Pallas kernels for 0%

commit v1 on v0

v1 whole, which is shorter than its diff:
```python
import functools

import jax
import jax.numpy as jnp
from jax import lax
from jax.experimental import pallas as pl
from jax.experimental.pallas import tpu as pltpu
from jax.sharding import PartitionSpec as P

STEPS = 16
MESH = pl.DeviceIdType.MESH
VM = pl.BlockSpec(memory_space=pltpu.VMEM)
SM = pl.BlockSpec(memory_space=pltpu.SMEM)
EXTRA = 16
BF = jnp.bfloat16
F32 = jnp.float32


def at(dp, z):
    return {"dp": dp, "tensor": z}


def enter(peers):
    barrier = pltpu.get_barrier_semaphore()
    for peer in peers:
        pl.semaphore_signal(barrier, inc=1, device_id=peer, device_id_type=MESH)
    pl.semaphore_wait(barrier, len(peers))


def chain_lengths(nt):
    half = nt // 2
    return {(0, 0): half, (0, 1): nt - 1 - half, (1, 0): nt - 1 - half, (1, 1): half}


def chain_order(nt):
    lengths = chain_lengths(nt)
    order = []
    for step in range(nt // 2):
        for turn in range(2):
            for side in range(2):
                kind = (turn + side) % 2
                if step < lengths[kind, side]:
                    order.append((kind, side, step))
    return order


CUTS = ((0, 640), (640, 512))


def pieces(kind):
    start, size = CUTS[kind]
    out = []
    while size > 0:
        step = min(size, 256)
        out.append((start, step))
        start, size = start + step, size - step
    return out


def head_kernel(
    nt,
    hid_i, w_i, pooled, hid_t, w_t, mrows,
    img_ext, img_unit, img_len, txt_low, txt_unit, txt_len,
    out_buf, in_buf, out_wide, in_wide, acc, hid_all, w_all,
    send_sem, recv_sem, hid_send, hid_recv, w_send, w_recv, pair_send, pair_recv,
):
    dp = lax.axis_index("dp")
    z = lax.axis_index("tensor")
    core = lax.rem(dp, 2)
    partner = dp + 1 - 2 * core
    right = lax.rem(z + 1, nt)
    left = lax.rem(z + nt - 1, nt)
    rows = pooled.shape[0]
    width = pooled.shape[1]
    enter([at(dp, lax.rem(z + away, nt)) for away in range(1, nt)] + [at(partner, z)])
    lengths = chain_lengths(nt)
    order = chain_order(nt)
    slots = {key: n for n, key in enumerate(order)}

    def hid_copy(away):
        dest = lax.rem(z + away, nt)
        return pltpu.make_async_remote_copy(
            src_ref=hid_t.at[:, pl.ds(pl.multiple_of(dest * rows, rows), rows)],
            dst_ref=hid_all.at[z],
            send_sem=hid_send.at[away], recv_sem=hid_recv.at[away],
            device_id=at(dp, dest), device_id_type=MESH,
        )

    ahead = lax.rem(z + 1 + core * (nt - 2), nt)
    hop = nt - 1 + 2 * core

    def w_copy(step):
        owner = lax.rem(z + (nt + hop) * step, nt)
        return pltpu.make_async_remote_copy(
            src_ref=w_t if step == 0 else w_all.at[owner],
            dst_ref=w_all.at[owner],
            send_sem=w_send.at[step], recv_sem=w_recv.at[step],
            device_id=at(dp, ahead), device_id_type=MESH,
        )

    def w_across(step):
        owner = lax.rem(z + (nt + hop) * step, nt)
        return pltpu.make_async_remote_copy(
            src_ref=w_all.at[owner], dst_ref=w_all.at[owner],
            send_sem=pair_send.at[step], recv_sem=pair_recv.at[step],
            device_id=at(partner, z), device_id_type=MESH,
        )

    half = nt // 2

    def w_turn(step):
        def turn():
            if step > 0:
                w_copy(step - 1).wait_recv()
                w_across(step).start()
            if step < half:
                if step == half - 1:
                    @pl.when(core == 0)
                    def _():
                        w_copy(step).start()
                else:
                    w_copy(step).start()
        if step == half:
            pl.when(core == 0)(turn)
        else:
            turn()

    def partial(dest, cols):
        block = hid_i[:, pl.ds(pl.multiple_of(dest * rows, rows), rows)]
        return lax.dot_general(
            block, w_i[:, cols], (((0,), (0,)), ((), ())), preferred_element_type=F32
        )

    def wide(n):
        kind, side, step = order[n]
        return step == lengths[kind, side] - 1

    def copy(n):
        kind, side, step = order[n]
        size = CUTS[kind][1]
        if wide(n):
            src = out_wide.at[2 * kind + side, :, pl.ds(0, size)]
            dst = in_wide.at[2 * kind + side, :, pl.ds(0, size)]
        else:
            src = out_buf.at[n, :, pl.ds(0, size)]
            dst = in_buf.at[n, :, pl.ds(0, size)]
        return pltpu.make_async_remote_copy(
            src_ref=src, dst_ref=dst, send_sem=send_sem.at[n], recv_sem=recv_sem.at[n],
            device_id=at(dp, right if side == 0 else left), device_id_type=MESH,
        )

    for away in range(1, nt):
        hid_copy(away).start()
    hid_all[z] = hid_t[:, pl.ds(pl.multiple_of(z * rows, rows), rows)]
    w_all[z] = w_t[...]

    for n, (kind, side, step) in enumerate(order):
        away = lengths[kind, side] - step
        dest = lax.rem(z + (away if side == 0 else nt - away), nt)
        before = None
        if step > 0:
            before = slots[kind, side, step - 1]
            copy(before).wait_recv()
        for start, size in pieces(kind):
            cols = pl.ds(start, size)
            local = pl.ds(start - CUTS[kind][0], size)
            value = partial(dest, cols)
            if before is not None:
                value = value + in_buf[before, :, local].astype(F32)
            if wide(n):
                out_wide[2 * kind + side, :, local] = value
            else:
                out_buf[n, :, local] = value.astype(BF)
        copy(n).start()
        if n in (1, 5, 9, 12):
            w_turn((1, 5, 9, 12).index(n))
    w_turn(half)

    squares = jnp.zeros((rows, 1), F32)
    for kind in range(2):
        for side in range(2):
            copy(slots[kind, side, lengths[kind, side] - 1]).wait_recv()
        for start, size in pieces(kind):
            cols = pl.ds(start, size)
            local = pl.ds(start - CUTS[kind][0], size)
            value = partial(z, cols)
            value = value + in_wide[2 * kind, :, local] + in_wide[2 * kind + 1, :, local]
            value = value + pooled[:, cols].astype(F32)
            acc[:, cols] = value
            squares = squares + jnp.sum(value * value, axis=1, keepdims=True)

    def finish(squares, unit_ref, len_ref, low_ref):
        length = jnp.sqrt(squares + 1e-06)
        len_ref[...] = length

        @pl.loop(0, width // 128)
        def _(t):
            cols = pl.ds(pl.multiple_of(t * 128, 128), 128)
            unit = acc[:, cols] / length
            unit_ref[:, cols] = unit
            low_ref[pl.ds(0, rows), cols] = unit.astype(BF)

    finish(squares, img_unit, img_len, img_ext)
    img_ext[pl.ds(rows, EXTRA), :] = jnp.zeros((EXTRA, width), BF)
    img_ext[pl.ds(rows, EXTRA), pl.ds(0, rows)] = mrows[...]

    for away in range(1, nt):
        hid_copy(away).wait_recv()
    for step in range(1, half):
        w_across(step).wait_recv()

    @pl.when(core == 1)
    def _():
        w_across(half).wait_recv()

    depth = hid_t.shape[0] * nt
    flat = hid_all[...].reshape(depth, rows)

    def txt_tile(t, squares):
        cols = pl.ds(pl.multiple_of(t * 384, 384), 384)
        value = lax.dot_general(
            flat, w_all[:, :, cols].reshape(depth, 384), (((0,), (0,)), ((), ())),
            preferred_element_type=F32,
        )
        acc[:, cols] = value
        return squares + jnp.sum(value * value, axis=1, keepdims=True)

    squares = lax.fori_loop(0, width // 384, txt_tile, jnp.zeros((rows, 1), F32))
    finish(squares, txt_unit, txt_len, txt_low)

    for n in range(len(order)):
        copy(n).wait_send()
    for away in range(1, nt):
        hid_copy(away).wait_send()
    for step in range(half - 1):
        w_copy(step).wait_send()
    for step in range(1, half):
        w_across(step).wait_send()

    @pl.when(core == 0)
    def _():
        w_copy(half - 1).wait_send()
        w_across(half).wait_send()


def head(nt, hid_i, w_i, pooled, hid_t, w_t, mrows):
    rows, width = pooled.shape
    items = len(chain_order(nt))
    most = CUTS[0][1]
    f = jax.ShapeDtypeStruct
    dma = pltpu.SemaphoreType.DMA
    return pl.pallas_call(
        functools.partial(head_kernel, nt),
        name="head",
        out_shape=(
            f((rows + EXTRA, width), BF),
            f((rows, width), F32),
            f((rows, 1), F32),
            f((rows, width), BF),
            f((rows, width), F32),
            f((rows, 1), F32),
        ),
        in_specs=[VM] * 6,
        out_specs=(VM,) * 6,
        scratch_shapes=[
            pltpu.VMEM((items, rows, most), BF),
            pltpu.VMEM((items, rows, most), BF),
            pltpu.VMEM((4, rows, most), F32),
            pltpu.VMEM((4, rows, most), F32),
            pltpu.VMEM((rows, width), F32),
            pltpu.VMEM((nt, hid_t.shape[0], rows), BF),
            pltpu.VMEM((nt, hid_t.shape[0], width), BF),
            dma((items,)), dma((items,)), dma((nt,)), dma((nt,)),
            dma((nt,)), dma((nt,)), dma((nt,)), dma((nt,)),
        ],
        compiler_params=pltpu.CompilerParams(
            collective_id=0, has_side_effects=True, vmem_limit_bytes=48 << 20
        ),
    )(hid_i, w_i, pooled, hid_t, w_t, mrows)


def column_of(dp, by, columns):
    return lax.rem(dp // 2 + (by % columns), columns) * 2 + lax.rem(dp, 2)


def spread_kernel(
    nt, columns, window,
    img, txt,
    imgs, txts,
    img_send, img_recv, send_sem, recv_sem, pair_send, pair_recv, local_sem,
):
    dp = lax.axis_index("dp")
    z = lax.axis_index("tensor")
    core = lax.rem(dp, 2)
    partner = dp + 1 - 2 * core
    right = lax.rem(z + 1, nt)
    left = lax.rem(z + nt - 1, nt)
    half = txt.shape[0] // 2
    peers = [at(dp, right), at(dp, left), at(partner, z)]
    for by in (window, window + 1):
        if by % columns:
            peers.append(at(column_of(dp, by, columns), z))
            peers.append(at(column_of(dp, -by, columns), z))
    enter(peers)

    lengths = chain_lengths(nt)
    order = chain_order(nt)
    slots = {key: n for n, key in enumerate(order)}

    image_copies = []
    for slot in range(2):
        by = window + slot
        if by % columns:
            c = pltpu.make_async_remote_copy(
                src_ref=img, dst_ref=imgs.at[slot],
                send_sem=img_send.at[slot], recv_sem=img_recv.at[slot],
                device_id=at(column_of(dp, -by, columns), z), device_id_type=MESH,
            )
        else:
            c = pltpu.make_async_copy(img, imgs.at[slot], img_recv.at[slot])
        image_copies.append(c)

    def part(owner, kind):
        return txts.at[core * nt + owner, pl.ds(kind * half, half)]

    def ring(n, owner, own):
        kind, side, step = order[n]
        src = txt.at[pl.ds(kind * half, half)] if own else part(owner, kind)
        return pltpu.make_async_remote_copy(
            src_ref=src, dst_ref=part(owner, kind),
            send_sem=send_sem.at[n], recv_sem=recv_sem.at[n],
            device_id=at(dp, right if side == 0 else left), device_id_type=MESH,
        )

    def across(n, owner, kind, own):
        src = txt.at[pl.ds(kind * half, half)] if own else part(owner, kind)
        return pltpu.make_async_remote_copy(
            src_ref=src, dst_ref=part(owner, kind),
            send_sem=pair_send.at[n], recv_sem=pair_recv.at[n],
            device_id=at(partner, z), device_id_type=MESH,
        )

    items = len(order)
    started = []
    pairs = []
    for n, (kind, side, step) in enumerate(order):
        back = step if side == 0 else nt - step
        owner = lax.rem(z + nt - back, nt)
        if step > 0:
            before = slots[kind, side, step - 1]
            ring(before, owner, step == 1).wait_recv()
        c = ring(n, owner, step == 0)
        c.start()
        started.append(c)
        if n == 1:
            for c in image_copies:
                c.start()
        if step > 0:
            c = across(before, owner, kind, False)
            c.start()
            pairs.append(c)
    own_pairs = []
    for kind in range(2):
        c = across(items + kind, z, kind, True)
        c.start()
        own_pairs.append(c)
    mine = pltpu.make_async_copy(txt, txts.at[core * nt + z], local_sem)
    mine.start()
    for (kind, side), length in lengths.items():
        n = slots[kind, side, length - 1]
        back = length if side == 0 else nt - length
        owner = lax.rem(z + nt - back, nt)
        ring(n, owner, False).wait_recv()
        c = across(n, owner, kind, False)
        c.start()
        pairs.append(c)
    for c in started:
        c.wait_send()
    for c in pairs + own_pairs + image_copies:
        c.wait()
    mine.wait()


def spread(nt, columns, window, img, txt):
    rows, width = txt.shape
    items = len(chain_order(nt))
    f = jax.ShapeDtypeStruct
    return pl.pallas_call(
        functools.partial(spread_kernel, nt, columns, window),
        name=f"spread_{window}",
        out_shape=(
            f((2, rows + EXTRA, width), BF),
            f((2 * nt, rows, width), BF),
        ),
        in_specs=[VM] * 2,
        out_specs=(VM,) * 2,
        scratch_shapes=[
            pltpu.SemaphoreType.DMA((2,)),
            pltpu.SemaphoreType.DMA((2,)),
            pltpu.SemaphoreType.DMA((items,)),
            pltpu.SemaphoreType.DMA((items,)),
            pltpu.SemaphoreType.DMA((items + 2,)),
            pltpu.SemaphoreType.DMA((items + 2,)),
            pltpu.SemaphoreType.DMA,
        ],
        compiler_params=pltpu.CompilerParams(
            collective_id=1 + window, has_side_effects=True, vmem_limit_bytes=48 << 20
        ),
    )(img, txt)


def pairs_kernel(
    nt,
    log_temp, bias, imgs, txts,
    img_part, txt_part,
    both, coefs, loss,
):
    dp = lax.axis_index("dp")
    z = lax.axis_index("tensor")
    mine = lax.rem(dp, 2) * nt + z
    first_block = (dp // 2) * (2 * nt)
    rows = txts.shape[1]
    width = txts.shape[2]
    blocks = txts.shape[0]
    tile = 384
    both[pl.ds(0, rows), :] = imgs[0, pl.ds(0, rows), :]
    both[pl.ds(rows, rows), :] = imgs[1, pl.ds(0, rows), :]
    scale = jnp.exp(jnp.full((1, rows), log_temp[0], F32))
    shift = jnp.full((1, rows), bias[0], F32)
    match = []
    for slot in range(2):
        high = imgs[slot, pl.ds(rows, 1), pl.ds(0, rows)].astype(F32)
        low = imgs[slot, pl.ds(rows + 1, 1), pl.ds(0, rows)].astype(F32)
        match.append((high * 256.0 + low).astype(jnp.int32))
    loss[...] = jnp.zeros_like(loss)

    @pl.loop(0, blocks)
    def _(j):
        block = txts[j]
        cosine = lax.dot_general(
            block, both[...], (((1,), (1,)), ((), ())), preferred_element_type=F32
        )
        early = j <= mine
        cosine = jnp.where(early, cosine[:, :rows], cosine[:, rows:])
        wanted = jnp.where(early, match[0], match[1])
        index = (first_block + j) * rows + lax.broadcasted_iota(jnp.int32, (rows, rows), 0)
        positive = index == wanted
        logit = scale * cosine + shift
        small = jnp.exp(-jnp.abs(logit))
        plus = jnp.maximum(logit, 0.0) + jnp.log1p(small)
        each = plus - jnp.where(positive, logit, 0.0)
        row = jnp.sum(each, axis=0, keepdims=True)
        zero = jnp.zeros_like(row)
        loss[pl.ds(0, 1), :] += jnp.where(early, row, zero)
        loss[pl.ds(1, 1), :] += jnp.where(early, zero, row)
        sig = jnp.where(logit >= 0, 1.0, small) / (1.0 + small)
        coef = (sig - positive.astype(F32)) * scale
        none = jnp.zeros_like(coef)
        turned = jnp.transpose(coef, (1, 0)).astype(BF)
        coef = jnp.concatenate(
            [jnp.where(early, coef, none), jnp.where(early, none, coef)], axis=1
        ).astype(BF)
        none = jnp.zeros_like(turned)
        cols = pl.ds(pl.multiple_of(j * rows, rows), rows)
        coefs[pl.ds(0, rows), cols] = jnp.where(early, turned, none)
        coefs[pl.ds(rows, rows), cols] = jnp.where(early, none, turned)
        for t in range(width // tile):
            c = pl.ds(t * tile, tile)
            txt_part[j, :, c] = jnp.dot(
                coef, both[:, c], preferred_element_type=F32
            ).astype(BF)

    @pl.loop(0, width // 128)
    def _(t):
        c = pl.ds(pl.multiple_of(t * 128, 128), 128)
        flat = txts[:, :, c].reshape(blocks * rows, 128)
        value = jnp.dot(coefs[...], flat, preferred_element_type=F32).astype(BF)
        img_part[0, pl.ds(0, rows), c] = value[:rows]
        img_part[1, pl.ds(0, rows), c] = value[rows:]

    for slot in range(2):
        whole = loss[pl.ds(slot, 1), :]
        high = whole.astype(BF).astype(F32)
        line = lax.broadcasted_iota(jnp.int32, (EXTRA, rows), 0)
        out = jnp.where(line == 0, high, jnp.where(line == 1, whole - high, 0.0))
        img_part[slot, pl.ds(rows, EXTRA), :] = jnp.zeros((EXTRA, width), BF)
        img_part[slot, pl.ds(rows, EXTRA), pl.ds(0, rows)] = out.astype(BF)


def pair_blocks(nt, log_temp, bias, imgs, txts):
    blocks, rows, width = txts.shape
    f = jax.ShapeDtypeStruct
    return pl.pallas_call(
        functools.partial(pairs_kernel, nt),
        name="pairs",
        out_shape=(
            f((2, rows + EXTRA, width), BF),
            f((blocks, rows, width), BF),
        ),
        in_specs=[SM, SM, VM, VM],
        out_specs=(VM,) * 2,
        scratch_shapes=[
            pltpu.VMEM((2 * rows, width), BF),
            pltpu.VMEM((2 * rows, blocks * rows), BF),
            pltpu.VMEM((8, rows), F32),
        ],
        compiler_params=pltpu.CompilerParams(vmem_limit_bytes=48 << 20),
    )(log_temp, bias, imgs, txts)


def gather_kernel(
    nt, columns, window,
    img_part, txt_part,
    img_back, txt_sum,
    other, out_buf, in_buf, out_wide, in_wide, img_send, img_recv, send_sem, recv_sem, pair_send, pair_recv,
):
    dp = lax.axis_index("dp")
    z = lax.axis_index("tensor")
    core = lax.rem(dp, 2)
    partner = dp + 1 - 2 * core
    right = lax.rem(z + 1, nt)
    left = lax.rem(z + nt - 1, nt)
    rows = txt_sum.shape[0]
    width = txt_sum.shape[1]
    half = rows // 2
    tile = 384
    peers = [at(dp, right), at(dp, left), at(partner, z)]
    for by in (window, window + 1):
        if by % columns:
            peers.append(at(column_of(dp, by, columns), z))
            peers.append(at(column_of(dp, -by, columns), z))
    enter(peers)

    lengths = chain_lengths(nt)
    order = chain_order(nt)
    slots = {key: n for n, key in enumerate(order)}

    def across(away):
        dest = lax.rem(z + away, nt)
        return pltpu.make_async_remote_copy(
            src_ref=txt_part.at[(1 - core) * nt + dest], dst_ref=other.at[dest],
            send_sem=pair_send.at[away], recv_sem=pair_recv.at[away],
            device_id=at(partner, z), device_id_type=MESH,
        )

    pair_order = []
    for kind, side, step in order:
        away = lengths[kind, side] - step
        away = away if side == 0 else nt - away
        if away not in pair_order:
            pair_order.append(away)
    pair_order.append(0)
    for away in pair_order:
        across(away).start()

    image_copies = []
    for slot in range(2):
        by = window + slot
        if by % columns:
            c = pltpu.make_async_remote_copy(
                src_ref=img_part.at[slot], dst_ref=img_back.at[slot],
                send_sem=img_send.at[slot], recv_sem=img_recv.at[slot],
                device_id=at(column_of(dp, by, columns), z), device_id_type=MESH,
            )
        else:
            c = pltpu.make_async_copy(img_part.at[slot], img_back.at[slot], img_recv.at[slot])
        c.start()
        image_copies.append(c)

    def wide(n):
        kind, side, step = order[n]
        return step == lengths[kind, side] - 1

    def copy(n):
        kind, side, step = order[n]
        return pltpu.make_async_remote_copy(
            src_ref=out_wide.at[2 * kind + side] if wide(n) else out_buf.at[n],
            dst_ref=in_wide.at[2 * kind + side] if wide(n) else in_buf.at[n],
            send_sem=send_sem.at[n], recv_sem=recv_sem.at[n],
            device_id=at(dp, right if side == 0 else left), device_id_type=MESH,
        )

    waited = []

    def both_cores(dest, lines, cols):
        own = txt_part[core * nt + dest, lines, cols].astype(F32)
        return own + other[dest, lines, cols].astype(F32)

    for n, (kind, side, step) in enumerate(order):
        away = lengths[kind, side] - step
        away = away if side == 0 else nt - away
        dest = lax.rem(z + away, nt)
        if away not in waited:
            across(away).wait_recv()
            waited.append(away)
        before = None
        if step > 0:
            before = slots[kind, side, step - 1]
            copy(before).wait_recv()

        @pl.loop(0, width // tile)
        def _(t, kind=kind, side=side, dest=dest, before=before, n=n):
            cols = pl.ds(pl.multiple_of(t * tile, tile), tile)
            value = both_cores(dest, pl.ds(kind * half, half), cols)
            if before is not None:
                value = value + in_buf[before, :, cols].astype(F32)
            if wide(n):
                out_wide[2 * kind + side, :, cols] = value
            else:
                out_buf[n, :, cols] = value.astype(BF)

        copy(n).start()

    across(0).wait_recv()
    for kind in range(2):
        last = []
        for side in range(2):
            n = slots[kind, side, lengths[kind, side] - 1]
            copy(n).wait_recv()
            last.append(n)

        @pl.loop(0, width // tile)
        def _(t, kind=kind, last=last):
            cols = pl.ds(pl.multiple_of(t * tile, tile), tile)
            value = both_cores(z, pl.ds(kind * half, half), cols)
            value = value + in_wide[2 * kind, :, cols] + in_wide[2 * kind + 1, :, cols]
            txt_sum[pl.ds(kind * half, half), cols] = value

    for n in range(len(order)):
        copy(n).wait_send()
    for away in pair_order:
        across(away).wait_send()
    for c in image_copies:
        c.wait()


def gather(nt, columns, window, img_part, txt_part):
    blocks, rows, width = txt_part.shape
    items = len(chain_order(nt))
    f = jax.ShapeDtypeStruct
    return pl.pallas_call(
        functools.partial(gather_kernel, nt, columns, window),
        name=f"gather_{window}",
        out_shape=(
            f((2, rows + EXTRA, width), BF),
            f((rows, width), F32),
        ),
        in_specs=[VM] * 2,
        out_specs=(VM,) * 2,
        scratch_shapes=[
            pltpu.VMEM((nt, rows, width), BF),
            pltpu.VMEM((items, rows // 2, width), BF),
            pltpu.VMEM((items, rows // 2, width), BF),
            pltpu.VMEM((4, rows // 2, width), F32),
            pltpu.VMEM((4, rows // 2, width), F32),
            pltpu.SemaphoreType.DMA((2,)),
            pltpu.SemaphoreType.DMA((2,)),
            pltpu.SemaphoreType.DMA((items,)),
            pltpu.SemaphoreType.DMA((items,)),
            pltpu.SemaphoreType.DMA((nt,)),
            pltpu.SemaphoreType.DMA((nt,)),
        ],
        compiler_params=pltpu.CompilerParams(
            collective_id=32 + window, has_side_effects=True, vmem_limit_bytes=48 << 20
        ),
    )(img_part, txt_part)


def body(
    img_hidden, img_down, img_pooled, txt_hidden, txt_proj, log_temp, bias, match, window_index
):
    nt = lax.axis_size("tensor")
    columns = lax.axis_size("dp") // 2
    rows, width = img_pooled.shape
    windows = columns
    window = window_index[0]
    line = lax.broadcasted_iota(jnp.int32, (EXTRA, rows), 0)
    mrows = jnp.where(
        line == 0, match[None, :] >> 8, jnp.where(line == 1, match[None, :] & 255, 0)
    ).astype(BF)
    img_ext, img_unit, img_len, txt_low, txt_unit, txt_len = head(
        nt, img_hidden.T, img_down, img_pooled, txt_hidden.T, txt_proj, mrows
    )
    imgs, txts = lax.switch(
        window,
        [functools.partial(spread, nt, columns, w) for w in range(windows)],
        img_ext, txt_low,
    )
    img_part, txt_part = pair_blocks(nt, log_temp, bias, imgs, txts)
    img_back, text_dunit = lax.switch(
        window,
        [functools.partial(gather, nt, columns, w) for w in range(windows)],
        img_part, txt_part,
    )
    back = img_back.astype(F32)
    image_dunit = back[0, :rows] + back[1, :rows]
    row_loss = jnp.sum(back[:, rows:rows + 2, :rows], axis=(0, 1))
    img_grad = (
        image_dunit - img_unit * jnp.sum(img_unit * image_dunit, axis=1, keepdims=True)
    ) / img_len
    txt_grad = (
        text_dunit - txt_unit * jnp.sum(txt_unit * text_dunit, axis=1, keepdims=True)
    ) / txt_len
    return (img_grad, txt_grad, row_loss)


def solution(mesh):
    in_specs = (
        P("dp", "tensor"),
        P("tensor", None),
        P(("dp", "tensor"), None),
        P("dp", "tensor"),
        P("tensor", None),
        P(),
        P(),
        P(("dp", "tensor")),
        P(),
    )
    out_specs = (P(("dp", "tensor"), None), P(("dp", "tensor"), None), P(("dp", "tensor")))
    return jax.shard_map(body, mesh=mesh, in_specs=in_specs, out_specs=out_specs, check_vma=False)
```

time: 493 us -> 161 us (0.33)
  waiting for transfers between devices: 347 us -> 0 us
  Pallas kernels: 0 us -> 148 us
  matrix products: 50.9 us -> 0 us
  starting transfers between devices: 48.7 us -> 0 us
  between operations: 16.3 us -> 2.62 us
  other arithmetic: 12 us -> 3.84 us
  local copies, waits for them, and re-layouts: 12.2 us -> 5.44 us
    ppermute x39 -> x0, waiting for transfers between devices: 238 us -> none  [shifted(): lax.ppermute(shard, axis, [(i, (i + by) % devices) for i in range(devices)])]
    pallas_call x0 -> x4, Pallas kernels: none -> 148 us  [the longest x1 62.4 us: head(): pl.pallas_call(functools.partial(head_kernel, nt), name='head', out_shape...]
    reduce_scatter x1 -> x0, waiting for transfers between devices: 109 us -> none  [body(): lax.psum_scatter(jnp.concatenate([jnp.dot(img_hidden, img_down, preferred...]
    dot_general x50 -> x0, matrix products: 50.9 us -> none  [the longest x16 25 us: pair_tile(): lax.dot_general(coef, image_low, (((0,), (0,)), ((), ())), preferred_elem...]
    ppermute x39 -> x0, starting transfers between devices: 48.6 us -> none  [shifted(): lax.ppermute(shard, axis, [(i, (i + by) % devices) for i in range(devices)])]
    while x14 -> x0, local copies, waits for them, and re-layouts: 10 us -> none
    concatenate x1 -> x0, other arithmetic: 6.7 us -> none  [body(): jnp.concatenate([jnp.dot(img_hidden, img_down, preferred_element_type=jnp...]
  transfers between devices with their start and end apart: 40 -> 0, of which waited for: 32 -> 0; matrix products, arithmetic and copies ran while one was open for 9% -> 0% of each run, Pallas kernels for 0% -> 0%
where the time goes in v1:
time: 161 us; the launch traced here: 160 us
  Pallas kernels  148 us (92%)
  local copies, waits for them, and re-layouts  5.44 us (3%)
  other arithmetic  3.84 us (2%)
  between operations  2.62 us (2%)
    pallas_call x1, Pallas kernels, head(): pl.pallas_call(functools.partial(head_kernel, nt), name='head', out_shape...  62.4 us
    pallas_call x1, Pallas kernels, gather(): pl.pallas_call(functools.partial(gather_kernel, nt, columns, window), nam...  35 us
    pallas_call x1, Pallas kernels, spread(): pl.pallas_call(functools.partial(spread_kernel, nt, columns, window), nam...  32.2 us
    pallas_call x1, Pallas kernels, pair_blocks(): pl.pallas_call(functools.partial(pairs_kernel, nt), name='pairs', out_sha...  18 us
    unnamed x10, local copies, waits for them, and re-layouts  5.44 us

profile of v1, /device:TPU:1, one launch (start us, length us, event | category | flops | bytes accessed | tf_op | source)
XLA Modules:
  0.0 159.8 jit_solution(729288689763008074)
XLA Ops:
  2.6 0.7 broadcast_shift-right-arithmetic_fusion
  3.2 0.1 select_convert_fusion.mrows
  3.3 0.0 copy-start
  3.3 1.3 copy-done
  4.6 0.0 copy-start.1
  4.6 1.2 copy-done.1
  5.9 0.0 copy-start.2
  5.9 1.0 copy-done.2
  6.8 0.0 copy-start.3
  6.8 1.0 copy-done.3
  7.8 0.0 copy-start.4
  7.8 1.0 copy-done.4
  8.8 62.4 %head.1 = (bf16[144,1152]{1,0:T(8,128)(2,1)S(1)}, f32[128,1152]{1,0:T(8,128)S(1)}, f32[128,1]{1,0:T(8,128)S(1)}, bf16[128,1152]{1,0:T(8,128)(2,1)S(1)}, f32[128,1152]{1,0:T(8,128)S(1)}, /*index=5*/f32[128,1]{1,0:T(8,128)S(1)}) custom-call(bf16[538,1024]{1,0:T(8,128)(2,1)S(1)} %bitcast.9, bf16[538,1152]{1,0:T(8,128)(2,1)S(1)} %copy-done, ...), custom_call_target="tpu_custom_call" | custom-call | tf_op jit(solution)/shard_map/head/pallas_call | solution.py:252
  71.2 0.1 reduce
  71.3 0.1 reduce.1
  71.4 32.5 %conditional.2 = ((bf16[2,144,1152]{2,1,0:T(8,128)(2,1)S(1)}, bf16[16,128,1152]{2,1,0:T(8,128)(2,1)})) conditional(s32[]{:T(128)} %bitcast, (bf16[144,1152]{1,0:T(8,128)(2,1)S(1)}, bf16[128,1152]{1,0:T(8,128)(2,1)S(1)}) %tuple.88, (bf16[144,1152]{1,0:T(8,128)(2,1)S(1)}, bf16[128,1152]{1,0:T(8,128)(2,1)S(1)}) %tuple.88, ...), branch_computations={%region_0.1_spmd, %region_1.2_spmd, %region_2.3_spmd, %region_3.4_... | conditional | bytes 8 | solution.py:684
  71.4 32.2 %spread_3.1 = (bf16[2,144,1152]{2,1,0:T(8,128)(2,1)S(1)}, bf16[16,128,1152]{2,1,0:T(8,128)(2,1)}) custom-call(bf16[144,1152]{1,0:T(8,128)(2,1)S(1)} %get-tuple-element.134.img, bf16[128,1152]{1,0:T(8,128)(2,1)S(1)} %get-tuple-element.135.txt), custom_call_target="tpu_custom_call" | custom-call | tf_op jit(solution)/shard_map/cond/branch_3_fun/spread_3/pallas_call | solution.py:388
  103.9 18.0 %pairs.1 = (bf16[2,144,1152]{2,1,0:T(8,128)(2,1)S(1)}, bf16[16,128,1152]{2,1,0:T(8,128)(2,1)S(1)}) custom-call(f32[1]{0:T(128)S(6)} %copy.76.log_temp, f32[1]{0:T(128)S(6)} %copy.77.bias, bf16[2,144,1152]{2,1,0:T(8,128)(2,1)S(1)} %get-tuple-element.207.imgs, bf16[16,128,1152]{2,1,0:T(8,128)(2,1)} %get-tuple-element.208.txts), custom_call_target="tpu_custom_call" | custom-call | tf_op jit(solution)/shard_map/pairs/pallas_call | solution.py:493
  121.9 35.1 %conditional.3 = ((bf16[2,144,1152]{2,1,0:T(8,128)(2,1)S(1)}, f32[128,1152]{1,0:T(8,128)S(1)})) conditional(s32[]{:T(128)} %bitcast, (bf16[2,144,1152]{2,1,0:T(8,128)(2,1)S(1)}, bf16[16,128,1152]{2,1,0:T(8,128)(2,1)S(1)}) %pairs.1, (bf16[2,144,1152]{2,1,0:T(8,128)(2,1)S(1)}, ...), branch_computations={%region_16.17_spmd, %region_17.18_spmd, %region_18.19_spmd, %regio... | conditional | bytes 8 | solution.py:690
  121.9 35.0 %gather_3.1 = (bf16[2,144,1152]{2,1,0:T(8,128)(2,1)S(1)}, f32[128,1152]{1,0:T(8,128)S(1)}) custom-call(bf16[2,144,1152]{2,1,0:T(8,128)(2,1)S(1)} %get-tuple-element.166.img_part, bf16[16,128,1152]{2,1,0:T(8,128)(2,1)S(1)} %get-tuple-element.167.txt_part), custom_call_target="tpu_custom_call" | custom-call | tf_op jit(solution)/shard_map/cond/branch_3_fun/gather_3/pallas_call | solution.py:641
  156.9 0.1 multiply_reduce_fusion
  157.1 1.0 subtract_divide_fusion
  158.1 0.1 convert_element_type.7
  158.2 0.2 multiply_reduce_fusion.1
  158.3 1.0 subtract_divide_fusion.1
  159.3 0.5 slice_reduce_fusion
  (1 shorter events, 0.0 us)
Async XLA Ops:
  3.3 1.3 copy-start
  4.6 1.2 copy-start.1
  5.9 1.0 copy-start.2
  6.8 1.0 copy-start.3
  7.8 1.0 copy-start.4

commit v2 on v1

v2 whole, which is shorter than its diff:
```python
import functools

import jax
import jax.numpy as jnp
from jax import lax
from jax.experimental import pallas as pl
from jax.experimental.pallas import tpu as pltpu
from jax.sharding import PartitionSpec as P

STEPS = 16
MESH = pl.DeviceIdType.MESH
VM = pl.BlockSpec(memory_space=pltpu.VMEM)
SM = pl.BlockSpec(memory_space=pltpu.SMEM)
EXTRA = 16
BF = jnp.bfloat16
F32 = jnp.float32


def at(dp, z):
    return {"dp": dp, "tensor": z}


def enter(peers):
    barrier = pltpu.get_barrier_semaphore()
    for peer in peers:
        pl.semaphore_signal(barrier, inc=1, device_id=peer, device_id_type=MESH)
    pl.semaphore_wait(barrier, len(peers))


def chain_lengths(nt):
    half = nt // 2
    return {(0, 0): half, (0, 1): nt - 1 - half, (1, 0): nt - 1 - half, (1, 1): half}


def chain_order(nt):
    lengths = chain_lengths(nt)
    order = []
    for step in range(nt // 2):
        for turn in range(2):
            for side in range(2):
                kind = (turn + side) % 2
                if step < lengths[kind, side]:
                    order.append((kind, side, step))
    return order


CUTS = ((0, 640), (640, 512))


def pieces(kind):
    start, size = CUTS[kind]
    out = []
    while size > 0:
        step = min(size, 256)
        out.append((start, step))
        start, size = start + step, size - step
    return out


def head_kernel(
    nt,
    hid_i, w_i, pooled, hid_t, w_t, mrows,
    img_ext, img_unit, img_len, txt_low, txt_unit, txt_len,
    out_buf, in_buf, out_wide, in_wide, acc, hid_all, w_all,
    send_sem, recv_sem, hid_send, hid_recv, w_send, w_recv, pair_send, pair_recv,
):
    dp = lax.axis_index("dp")
    z = lax.axis_index("tensor")
    core = lax.rem(dp, 2)
    partner = dp + 1 - 2 * core
    right = lax.rem(z + 1, nt)
    left = lax.rem(z + nt - 1, nt)
    rows = pooled.shape[0]
    width = pooled.shape[1]
    enter([at(dp, lax.rem(z + away, nt)) for away in range(1, nt)] + [at(partner, z)])
    lengths = chain_lengths(nt)
    order = chain_order(nt)
    slots = {key: n for n, key in enumerate(order)}

    def hid_copy(away):
        dest = lax.rem(z + away, nt)
        return pltpu.make_async_remote_copy(
            src_ref=hid_t.at[:, pl.ds(pl.multiple_of(dest * rows, rows), rows)],
            dst_ref=hid_all.at[z],
            send_sem=hid_send.at[away], recv_sem=hid_recv.at[away],
            device_id=at(dp, dest), device_id_type=MESH,
        )

    ahead = lax.rem(z + 1 + core * (nt - 2), nt)
    hop = nt - 1 + 2 * core

    def w_copy(step):
        owner = lax.rem(z + (nt + hop) * step, nt)
        return pltpu.make_async_remote_copy(
            src_ref=w_t if step == 0 else w_all.at[owner],
            dst_ref=w_all.at[owner],
            send_sem=w_send.at[step], recv_sem=w_recv.at[step],
            device_id=at(dp, ahead), device_id_type=MESH,
        )

    def w_across(step):
        owner = lax.rem(z + (nt + hop) * step, nt)
        return pltpu.make_async_remote_copy(
            src_ref=w_all.at[owner], dst_ref=w_all.at[owner],
            send_sem=pair_send.at[step], recv_sem=pair_recv.at[step],
            device_id=at(partner, z), device_id_type=MESH,
        )

    half = nt // 2

    def w_turn(step):
        def turn():
            if step > 0:
                w_copy(step - 1).wait_recv()
                w_across(step).start()
            if step < half:
                if step == half - 1:
                    @pl.when(core == 0)
                    def _():
                        w_copy(step).start()
                else:
                    w_copy(step).start()
        if step == half:
            pl.when(core == 0)(turn)
        else:
            turn()

    def partial(dest, cols):
        block = hid_i[:, pl.ds(pl.multiple_of(dest * rows, rows), rows)]
        return lax.dot_general(
            block, w_i[:, cols], (((0,), (0,)), ((), ())), preferred_element_type=F32
        )

    def wide(n):
        kind, side, step = order[n]
        return step == lengths[kind, side] - 1

    def copy(n):
        kind, side, step = order[n]
        size = CUTS[kind][1]
        if wide(n):
            src = out_wide.at[2 * kind + side, :, pl.ds(0, size)]
            dst = in_wide.at[2 * kind + side, :, pl.ds(0, size)]
        else:
            src = out_buf.at[n, :, pl.ds(0, size)]
            dst = in_buf.at[n, :, pl.ds(0, size)]
        return pltpu.make_async_remote_copy(
            src_ref=src, dst_ref=dst, send_sem=send_sem.at[n], recv_sem=recv_sem.at[n],
            device_id=at(dp, right if side == 0 else left), device_id_type=MESH,
        )

    for away in range(1, nt):
        hid_copy(away).start()
    hid_all[z] = hid_t[:, pl.ds(pl.multiple_of(z * rows, rows), rows)]
    w_all[z] = w_t[...]

    for n, (kind, side, step) in enumerate(order):
        away = lengths[kind, side] - step
        dest = lax.rem(z + (away if side == 0 else nt - away), nt)
        before = None
        if step > 0:
            before = slots[kind, side, step - 1]
            copy(before).wait_recv()
        for start, size in pieces(kind):
            cols = pl.ds(start, size)
            local = pl.ds(start - CUTS[kind][0], size)
            value = partial(dest, cols)
            if before is not None:
                value = value + in_buf[before, :, local].astype(F32)
            if wide(n):
                out_wide[2 * kind + side, :, local] = value
            else:
                out_buf[n, :, local] = value.astype(BF)
        copy(n).start()
        if n in (1, 5, 9, 12):
            w_turn((1, 5, 9, 12).index(n))
    w_turn(half)

    squares = jnp.zeros((rows, 1), F32)
    for kind in range(2):
        for side in range(2):
            copy(slots[kind, side, lengths[kind, side] - 1]).wait_recv()
        for start, size in pieces(kind):
            cols = pl.ds(start, size)
            local = pl.ds(start - CUTS[kind][0], size)
            value = partial(z, cols)
            value = value + in_wide[2 * kind, :, local] + in_wide[2 * kind + 1, :, local]
            value = value + pooled[:, cols].astype(F32)
            acc[:, cols] = value
            squares = squares + jnp.sum(value * value, axis=1, keepdims=True)

    def finish(squares, unit_ref, len_ref, low_ref):
        length = jnp.sqrt(squares + 1e-06)
        len_ref[...] = length

        @pl.loop(0, width // 128)
        def _(t):
            cols = pl.ds(pl.multiple_of(t * 128, 128), 128)
            unit = acc[:, cols] / length
            unit_ref[:, cols] = unit
            low_ref[pl.ds(0, rows), cols] = unit.astype(BF)

    finish(squares, img_unit, img_len, img_ext)
    img_ext[pl.ds(rows, EXTRA), :] = jnp.zeros((EXTRA, width), BF)
    img_ext[pl.ds(rows, EXTRA), pl.ds(0, rows)] = mrows[...]

    for away in range(1, nt):
        hid_copy(away).wait_recv()
    for step in range(1, half):
        w_across(step).wait_recv()

    @pl.when(core == 1)
    def _():
        w_across(half).wait_recv()

    depth = hid_t.shape[0] * nt
    flat = hid_all[...].reshape(depth, rows)

    def txt_tile(t, squares):
        cols = pl.ds(pl.multiple_of(t * 384, 384), 384)
        value = lax.dot_general(
            flat, w_all[:, :, cols].reshape(depth, 384), (((0,), (0,)), ((), ())),
            preferred_element_type=F32,
        )
        acc[:, cols] = value
        return squares + jnp.sum(value * value, axis=1, keepdims=True)

    squares = lax.fori_loop(0, width // 384, txt_tile, jnp.zeros((rows, 1), F32))
    finish(squares, txt_unit, txt_len, txt_low)

    for n in range(len(order)):
        copy(n).wait_send()
    for away in range(1, nt):
        hid_copy(away).wait_send()
    for step in range(half - 1):
        w_copy(step).wait_send()
    for step in range(1, half):
        w_across(step).wait_send()

    @pl.when(core == 0)
    def _():
        w_copy(half - 1).wait_send()
        w_across(half).wait_send()


def head(nt, hid_i, w_i, pooled, hid_t, w_t, mrows):
    rows, width = pooled.shape
    items = len(chain_order(nt))
    most = CUTS[0][1]
    f = jax.ShapeDtypeStruct
    dma = pltpu.SemaphoreType.DMA
    return pl.pallas_call(
        functools.partial(head_kernel, nt),
        name="head",
        out_shape=(
            f((rows + EXTRA, width), BF),
            f((rows, width), F32),
            f((rows, 1), F32),
            f((rows, width), BF),
            f((rows, width), F32),
            f((rows, 1), F32),
        ),
        in_specs=[VM] * 6,
        out_specs=(VM,) * 6,
        scratch_shapes=[
            pltpu.VMEM((items, rows, most), BF),
            pltpu.VMEM((items, rows, most), BF),
            pltpu.VMEM((4, rows, most), F32),
            pltpu.VMEM((4, rows, most), F32),
            pltpu.VMEM((rows, width), F32),
            pltpu.VMEM((nt, hid_t.shape[0], rows), BF),
            pltpu.VMEM((nt, hid_t.shape[0], width), BF),
            dma((items,)), dma((items,)), dma((nt,)), dma((nt,)),
            dma((nt,)), dma((nt,)), dma((nt,)), dma((nt,)),
        ],
        compiler_params=pltpu.CompilerParams(
            collective_id=0, has_side_effects=True, vmem_limit_bytes=48 << 20
        ),
    )(hid_i, w_i, pooled, hid_t, w_t, mrows)


def column_of(dp, by, columns):
    return lax.rem(dp // 2 + (by % columns), columns) * 2 + lax.rem(dp, 2)


def place(nt, rel):
    half = nt // 2
    return 2 * (rel - half) if rel >= half else 2 * (half - 1 - rel) + 1


def window_kernel(
    nt, columns, window,
    log_temp, bias, img, txt,
    img_back, txt_sum,
    imgs, txts, both, cosines, picked, turned_coefs, img_sum, loss,
    img_part, own, mate, other, out_buf, in_buf,
    img_send, img_recv, back_send, back_recv, send_sem, recv_sem, pair_send, pair_recv,
    sum_send, sum_recv, mate_send, mate_recv, local_sem,
):
    dp = lax.axis_index("dp")
    z = lax.axis_index("tensor")
    core = lax.rem(dp, 2)
    partner = dp + 1 - 2 * core
    right = lax.rem(z + 1, nt)
    left = lax.rem(z + nt - 1, nt)
    rows, width = txt.shape
    part = rows // 2
    groups = nt // 2
    peers = [at(dp, right), at(dp, left), at(partner, z)]
    for by in (window, window + 1):
        if by % columns:
            peers.append(at(column_of(dp, by, columns), z))
            peers.append(at(column_of(dp, -by, columns), z))
    enter(peers)

    lengths = chain_lengths(nt)
    order = chain_order(nt)
    items = len(order)
    slots = {key: n for n, key in enumerate(order)}

    def ring(n):
        kind, side, step = order[n]
        rel = (nt - step) % nt if side == 0 else step
        there = (rel + nt - 1) % nt if side == 0 else rel + 1
        lines = pl.ds(kind * part, part)
        return pltpu.make_async_remote_copy(
            src_ref=txt.at[lines] if step == 0 else txts.at[2 * place(nt, rel), lines],
            dst_ref=txts.at[2 * place(nt, there), lines],
            send_sem=send_sem.at[n], recv_sem=recv_sem.at[n],
            device_id=at(dp, right if side == 0 else left), device_id_type=MESH,
        )

    def across(rel, kind):
        lines = pl.ds(kind * part, part)
        p = place(nt, rel)
        return pltpu.make_async_remote_copy(
            src_ref=txt.at[lines] if rel == 0 else txts.at[2 * p, lines],
            dst_ref=txts.at[2 * p + 1, lines],
            send_sem=pair_send.at[2 * rel + kind], recv_sem=pair_recv.at[2 * rel + kind],
            device_id=at(partner, z), device_id_type=MESH,
        )

    def piece(sends, recvs, n):
        return pltpu.make_async_remote_copy(
            src_ref=txt.at[pl.ds(0, part)], dst_ref=txts.at[0, pl.ds(0, part)],
            send_sem=sends.at[n], recv_sem=recvs.at[n],
            device_id=at(partner, z), device_id_type=MESH,
        )

    def image_copy(out, slot):
        by = window + slot
        if out:
            src, dst, sems, step = img, imgs.at[slot], (img_send, img_recv), -by
        else:
            src, dst, sems, step = img_part.at[slot], img_back.at[slot], (back_send, back_recv), by
        if by % columns == 0:
            return pltpu.make_async_copy(src, dst, sems[1].at[slot])
        return pltpu.make_async_remote_copy(
            src_ref=src, dst_ref=dst, send_sem=sems[0].at[slot], recv_sem=sems[1].at[slot],
            device_id=at(column_of(dp, step, columns), z), device_id_type=MESH,
        )

    def arrived(n):
        kind, side, step = order[n]
        rel = nt - 1 - step if side == 0 else step + 1
        ring(n).wait_recv()
        across(rel, kind).start()

    for n, (kind, side, step) in enumerate(order):
        if step > 0:
            arrived(slots[kind, side, step - 1])
        ring(n).start()
        if n == 1:
            image_copy(True, 0).start()
            image_copy(True, 1).start()
        if n == 3:
            across(0, 0).start()
            across(0, 1).start()
    mine = pltpu.make_async_copy(txt, txts.at[2 * place(nt, 0)], local_sem)
    mine.start()
    for (kind, side), length in lengths.items():
        if length < nt // 2:
            arrived(slots[kind, side, length - 1])

    for slot in range(2):
        image_copy(True, slot).wait()
        both[pl.ds(slot * rows, rows), :] = imgs[slot, pl.ds(0, rows), :]
    mine.wait()
    scale = jnp.exp(jnp.full((1, rows), log_temp[0], F32))
    shift = jnp.full((1, rows), bias[0], F32)
    match = []
    for slot in range(2):
        high = imgs[slot, pl.ds(rows, 1), pl.ds(0, rows)].astype(F32)
        low = imgs[slot, pl.ds(rows + 1, 1), pl.ds(0, rows)].astype(F32)
        match.append((high * 256.0 + low).astype(jnp.int32))
    loss[...] = jnp.zeros_like(loss)
    img_sum[...] = jnp.zeros_like(img_sum)
    number = core * nt + z
    first_block = (dp // 2) * (2 * nt)

    def mates(g):
        return pltpu.make_async_remote_copy(
            src_ref=mate.at[pl.ds(2 * g, 2)], dst_ref=other.at[pl.ds(2 * g, 2)],
            send_sem=mate_send.at[g], recv_sem=mate_recv.at[g],
            device_id=at(partner, z), device_id_type=MESH,
        )

    far = nt // 2

    @pl.loop(0, 2 * far)
    def _(n):
        piece(pair_send, pair_recv, n).wait_recv()

    @pl.loop(2 * far + 2, 2 * nt)
    def _(n):
        piece(pair_send, pair_recv, n).wait_recv()

    @pl.loop(0, groups)
    def _(turn):
        g = groups - 1 - turn

        @pl.when(turn == groups - 1)
        def _():
            arrived(slots[0, 0, far - 1])
            arrived(slots[1, 1, far - 1])
            for kind in range(2):
                across(far, kind).wait_recv()

        @pl.loop(0, 2)
        def _(h):
            block = txts[pl.ds(4 * g + 2 * h, 2)].reshape(2 * rows, width)
            cosines[pl.ds(pl.multiple_of(2 * h * rows, 2 * rows), 2 * rows), :] = lax.dot_general(
                block, both[...], (((1,), (1,)), ((), ())), preferred_element_type=F32
            )

        @pl.loop(0, 4)
        def _(b):
            rel = lax.select(b < 2, groups + g, groups - 1 - g)
            owner = lax.rem(z + rel, nt)
            text_core = lax.rem(core + b, 2)
            j = text_core * nt + owner
            lines = pl.ds(pl.multiple_of(b * rows, rows), rows)
            early = j <= number
            cosine = jnp.where(
                early, cosines[lines, pl.ds(0, rows)], cosines[lines, pl.ds(rows, rows)]
            )
            wanted = jnp.where(early, match[0], match[1])
            index = (first_block + j) * rows + lax.broadcasted_iota(jnp.int32, (rows, rows), 0)
            positive = index == wanted
            logit = scale * cosine + shift
            small = jnp.exp(-jnp.abs(logit))
            plus = jnp.maximum(logit, 0.0) + jnp.log1p(small)
            each = plus - jnp.where(positive, logit, 0.0)
            row = jnp.sum(each, axis=0, keepdims=True)
            zero = jnp.zeros_like(row)
            loss[pl.ds(0, 1), :] += jnp.where(early, row, zero)
            loss[pl.ds(1, 1), :] += jnp.where(early, zero, row)
            sig = jnp.where(logit >= 0, 1.0, small) / (1.0 + small)
            coef = (sig - positive.astype(F32)) * scale
            none = jnp.zeros_like(coef)
            turned = jnp.transpose(coef, (1, 0)).astype(BF)
            picked[lines, :] = jnp.concatenate(
                [jnp.where(early, coef, none), jnp.where(early, none, coef)], axis=1
            ).astype(BF)
            none = jnp.zeros_like(turned)
            cols = pl.ds(pl.multiple_of(b * rows, rows), rows)
            turned_coefs[pl.ds(0, rows), cols] = jnp.where(early, turned, none)
            turned_coefs[pl.ds(rows, rows), cols] = jnp.where(early, none, turned)

        @pl.loop(0, width // 384)
        def _(t):
            c = pl.ds(pl.multiple_of(t * 384, 384), 384)
            value = jnp.dot(picked[...], both[:, c], preferred_element_type=F32)
            for i in range(2):
                own[2 * g + i, :, c] = value[2 * i * rows:(2 * i + 1) * rows]
                mate[2 * g + i, :, c] = value[(2 * i + 1) * rows:(2 * i + 2) * rows].astype(BF)
            flat = txts[pl.ds(4 * g, 4), :, c].reshape(4 * rows, 384)
            img_sum[:, c] += jnp.dot(turned_coefs[...], flat, preferred_element_type=F32)

        mates(g).start()

    def sums(n):
        kind, side, step = order[n]
        return pltpu.make_async_remote_copy(
            src_ref=out_buf.at[n], dst_ref=in_buf.at[n],
            send_sem=sum_send.at[n], recv_sem=sum_recv.at[n],
            device_id=at(dp, right if side == 0 else left), device_id_type=MESH,
        )

    def image_sums():
        @pl.loop(0, width // 128)
        def _(t):
            c = pl.ds(pl.multiple_of(t * 128, 128), 128)
            for slot in range(2):
                img_part[slot, pl.ds(0, rows), c] = img_sum[pl.ds(slot * rows, rows), c].astype(BF)

        for slot in range(2):
            whole = loss[pl.ds(slot, 1), :]
            high = whole.astype(BF).astype(F32)
            line = lax.broadcasted_iota(jnp.int32, (EXTRA, rows), 0)
            out = jnp.where(line == 0, high, jnp.where(line == 1, whole - high, 0.0))
            img_part[slot, pl.ds(rows, EXTRA), :] = jnp.zeros((EXTRA, width), BF)
            img_part[slot, pl.ds(rows, EXTRA), pl.ds(0, rows)] = out.astype(BF)
            image_copy(False, slot).start()

    @pl.loop(0, groups)
    def _(g):
        mates(g).wait_recv()

    for n, (kind, side, step) in enumerate(order):
        away = lengths[kind, side] - step
        p = place(nt, away if side == 0 else nt - away)
        before = None
        if step > 0:
            before = slots[kind, side, step - 1]
            sums(before).wait_recv()

        @pl.loop(0, width // 128)
        def _(t, kind=kind, side=side, p=p, before=before, n=n):
            c = pl.ds(pl.multiple_of(t * 128, 128), 128)
            lines = pl.ds(kind * part, part)
            value = own[p, lines, c] + other[p, lines, c].astype(F32)
            if before is not None:
                value = value + in_buf[before, :, c].astype(F32)
            out_buf[n, :, c] = value.astype(BF)

        sums(n).start()
        if n == 3:
            image_sums()

    for kind in range(2):
        last = [slots[kind, side, lengths[kind, side] - 1] for side in range(2)]
        for n in last:
            sums(n).wait_recv()

        @pl.loop(0, width // 128)
        def _(t, kind=kind, last=last):
            c = pl.ds(pl.multiple_of(t * 128, 128), 128)
            lines = pl.ds(kind * part, part)
            p = place(nt, 0)
            value = own[p, lines, c] + other[p, lines, c].astype(F32)
            for n in last:
                value = value + in_buf[n, :, c].astype(F32)
            txt_sum[lines, c] = value

    @pl.loop(0, items)
    def _(n):
        piece(send_sem, recv_sem, n).wait_send()
        piece(sum_send, sum_recv, n).wait_send()

    @pl.loop(0, 2 * nt)
    def _(n):
        piece(pair_send, pair_recv, n).wait_send()

    @pl.loop(0, groups)
    def _(g):
        mates(g).wait_send()

    for slot in range(2):
        image_copy(False, slot).wait()


def window_pass(nt, columns, window, log_temp, bias, img, txt):
    rows, width = txt.shape
    items = len(chain_order(nt))
    blocks = 2 * nt
    f = jax.ShapeDtypeStruct
    dma = pltpu.SemaphoreType.DMA
    ext = (2, rows + EXTRA, width)
    return pl.pallas_call(
        functools.partial(window_kernel, nt, columns, window),
        name=f"window_{window}",
        out_shape=(f(ext, BF), f((rows, width), F32)),
        in_specs=[SM, SM, VM, VM],
        out_specs=(VM,) * 2,
        scratch_shapes=[
            pltpu.VMEM(ext, BF),
            pltpu.VMEM((blocks, rows, width), BF),
            pltpu.VMEM((2 * rows, width), BF),
            pltpu.VMEM((4 * rows, 2 * rows), F32),
            pltpu.VMEM((4 * rows, 2 * rows), BF),
            pltpu.VMEM((2 * rows, 4 * rows), BF),
            pltpu.VMEM((2 * rows, width), F32),
            pltpu.VMEM((8, rows), F32),
            pltpu.VMEM(ext, BF),
            pltpu.VMEM((nt, rows, width), F32),
            pltpu.VMEM((nt, rows, width), BF),
            pltpu.VMEM((nt, rows, width), BF),
            pltpu.VMEM((items, rows // 2, width), BF),
            pltpu.VMEM((items, rows // 2, width), BF),
            dma((2,)), dma((2,)), dma((2,)), dma((2,)),
            dma((items,)), dma((items,)), dma((2 * nt,)), dma((2 * nt,)),
            dma((items,)), dma((items,)), dma((nt // 2,)), dma((nt // 2,)), dma,
        ],
        compiler_params=pltpu.CompilerParams(
            collective_id=1 + window, has_side_effects=True, vmem_limit_bytes=56 << 20
        ),
    )(log_temp, bias, img, txt)


def body(
    img_hidden, img_down, img_pooled, txt_hidden, txt_proj, log_temp, bias, match, window_index
):
    nt = lax.axis_size("tensor")
    columns = lax.axis_size("dp") // 2
    rows, width = img_pooled.shape
    windows = columns
    window = window_index[0]
    line = lax.broadcasted_iota(jnp.int32, (EXTRA, rows), 0)
    mrows = jnp.where(
        line == 0, match[None, :] >> 8, jnp.where(line == 1, match[None, :] & 255, 0)
    ).astype(BF)
    img_ext, img_unit, img_len, txt_low, txt_unit, txt_len = head(
        nt, img_hidden.T, img_down, img_pooled, txt_hidden.T, txt_proj, mrows
    )
    img_back, text_dunit = lax.switch(
        window,
        [functools.partial(window_pass, nt, columns, w) for w in range(windows)],
        log_temp, bias, img_ext, txt_low,
    )
    back = img_back.astype(F32)
    image_dunit = back[0, :rows] + back[1, :rows]
    row_loss = jnp.sum(back[:, rows:rows + 2, :rows], axis=(0, 1))
    img_grad = (
        image_dunit - img_unit * jnp.sum(img_unit * image_dunit, axis=1, keepdims=True)
    ) / img_len
    txt_grad = (
        text_dunit - txt_unit * jnp.sum(txt_unit * text_dunit, axis=1, keepdims=True)
    ) / txt_len
    return (img_grad, txt_grad, row_loss)


def solution(mesh):
    in_specs = (
        P("dp", "tensor"),
        P("tensor", None),
        P(("dp", "tensor"), None),
        P("dp", "tensor"),
        P("tensor", None),
        P(),
        P(),
        P(("dp", "tensor")),
        P(),
    )
    out_specs = (P(("dp", "tensor"), None), P(("dp", "tensor"), None), P(("dp", "tensor")))
    return jax.shard_map(body, mesh=mesh, in_specs=in_specs, out_specs=out_specs, check_vma=False)
```

time: 161 us -> 144 us (0.89)
  Pallas kernels: 148 us -> 131 us
    pallas_call x3 -> x1, Pallas kernels: 85.2 us -> 68.9 us  [window_pass(): pl.pallas_call(functools.partial(window_kernel, nt, columns, window), nam...]
where the time goes in v2:
time: 144 us; the launch traced here: 142 us
  Pallas kernels  131 us (91%)
  local copies, waits for them, and re-layouts  5.44 us (4%)
  other arithmetic  3.84 us (3%)
    pallas_call x1, Pallas kernels, window_pass(): pl.pallas_call(functools.partial(window_kernel, nt, columns, window), nam...  68.9 us
    pallas_call x1, Pallas kernels, head(): pl.pallas_call(functools.partial(head_kernel, nt), name='head', out_shape...  62.4 us
    unnamed x10, local copies, waits for them, and re-layouts  5.44 us

profile of v2, /device:TPU:1, one launch (start us, length us, event | category | flops | bytes accessed | tf_op | source)
XLA Modules:
  0.0 142.4 jit_solution(15076662640290832040)
XLA Ops:
  1.3 0.7 broadcast_shift-right-arithmetic_fusion
  1.9 0.1 select_convert_fusion.mrows
  2.0 0.0 copy-start
  2.0 1.3 copy-done
  3.3 0.0 copy-start.1
  3.3 1.2 copy-done.1
  4.6 0.0 copy-start.2
  4.6 1.0 copy-done.2
  5.5 0.0 copy-start.3
  5.5 1.0 copy-done.3
  6.5 0.0 copy-start.4
  6.5 1.0 copy-done.4
  7.5 62.4 %head.1 = (bf16[144,1152]{1,0:T(8,128)(2,1)S(1)}, f32[128,1152]{1,0:T(8,128)S(1)}, f32[128,1]{1,0:T(8,128)S(1)}, bf16[128,1152]{1,0:T(8,128)(2,1)S(1)}, f32[128,1152]{1,0:T(8,128)S(1)}, /*index=5*/f32[128,1]{1,0:T(8,128)S(1)}) custom-call(bf16[538,1024]{1,0:T(8,128)(2,1)S(1)} %bitcast.9, bf16[538,1152]{1,0:T(8,128)(2,1)S(1)} %copy-done, ...), custom_call_target="tpu_custom_call" | custom-call | tf_op jit(solution)/shard_map/head/pallas_call | solution.py:252
  69.9 0.1 reduce
  70.0 0.1 reduce.1
  70.1 69.5 %conditional.1 = ((bf16[2,144,1152]{2,1,0:T(8,128)(2,1)S(1)}, f32[128,1152]{1,0:T(8,128)S(1)})) conditional(s32[]{:T(128)} %bitcast, (f32[1]{0:T(128)}, f32[1]{0:T(128)}, bf16[144,1152]{1,0:T(8,128)(2,1)S(1)}, bf16[128,1152]{1,0:T(8,128)(2,1)S(1)}) %tuple.56, (f32[1]{0:T(128)}, f32[1]{0:T(128)}, ...), branch_computations={%region_0.1_spmd, %region_1.2_spmd, %region_2.3_spmd, %region_3.4_... | conditional | bytes 8 | solution.py:616
  70.3 68.9 %window_8.1 = (bf16[2,144,1152]{2,1,0:T(8,128)(2,1)S(1)}, f32[128,1152]{1,0:T(8,128)S(1)}) custom-call(f32[1]{0:T(128)} %get-tuple-element.160.log_temp, f32[1]{0:T(128)} %get-tuple-element.161.bias, bf16[144,1152]{1,0:T(8,128)(2,1)S(1)} %get-tuple-element.162.img, bf16[128,1152]{1,0:T(8,128)(2,1)S(1)} %get-tuple-element.163.txt), custom_call_target="tpu_custom_call" | custom-call | tf_op jit(solution)/shard_map/cond/branch_8_fun/window_8/pallas_call | solution.py:570
  139.5 0.1 multiply_reduce_fusion
  139.7 1.0 subtract_divide_fusion
  140.7 0.1 convert_element_type.7
  140.8 0.2 multiply_reduce_fusion.1
  140.9 1.0 subtract_divide_fusion.1
  141.9 0.5 slice_reduce_fusion
  (1 shorter events, 0.0 us)
Async XLA Ops:
  2.0 1.3 copy-start
  3.3 1.2 copy-start.1
  4.6 1.0 copy-start.2
  5.5 1.0 copy-start.3
  6.5 1.0 copy-start.4

commit v3 on v2

--- a/solution.py
+++ b/solution.py
@@ -10,6 +10,7 @@
 STEPS = 16
 MESH = pl.DeviceIdType.MESH
 VM = pl.BlockSpec(memory_space=pltpu.VMEM)
+HB = pl.BlockSpec(memory_space=pltpu.HBM)
 SM = pl.BlockSpec(memory_space=pltpu.SMEM)
 EXTRA = 16
 BF = jnp.bfloat16
@@ -58,21 +59,39 @@
 
 
 def head_kernel(
-    nt,
-    hid_i, w_i, pooled, hid_t, w_t, mrows,
+    nt, columns,
+    hid_i_hbm, w_i_hbm, pooled_hbm, hid_t_hbm, w_t_hbm, mrows,
     img_ext, img_unit, img_len, txt_low, txt_unit, txt_len,
     out_buf, in_buf, out_wide, in_wide, acc, hid_all, w_all,
+    hid_i, w_i, pooled, hid_t, w_t,
     send_sem, recv_sem, hid_send, hid_recv, w_send, w_recv, pair_send, pair_recv,
+    slab_send, slab_recv, load_sem,
 ):
     dp = lax.axis_index("dp")
     z = lax.axis_index("tensor")
     core = lax.rem(dp, 2)
     partner = dp + 1 - 2 * core
+    column = dp // 2
     right = lax.rem(z + 1, nt)
     left = lax.rem(z + nt - 1, nt)
     rows = pooled.shape[0]
     width = pooled.shape[1]
-    enter([at(dp, lax.rem(z + away, nt)) for away in range(1, nt)] + [at(partner, z)])
+    loads = [
+        pltpu.make_async_copy(src, dst, load_sem.at[n])
+        for n, (src, dst) in enumerate((
+            (hid_t_hbm, hid_t), (w_t_hbm, w_t), (hid_i_hbm, hid_i), (w_i_hbm, w_i),
+            (pooled_hbm, pooled),
+        ))
+    ]
+    for load in loads:
+        load.start()
+    enter(
+        [at(dp, lax.rem(z + away, nt)) for away in range(1, nt)] + [at(partner, z)]
+        + [at(lax.rem(column + 4 * by, columns) * 2 + core, z) for by in range(1, columns // 4)]
+        + [at((column - lax.rem(column, 4) + lax.rem(column + by, 4)) * 2 + core, z) for by in range(1, 4)]
+    )
+    for load in loads:
+        load.wait()
     lengths = chain_lengths(nt)
     order = chain_order(nt)
     slots = {key: n for n, key in enumerate(order)}
@@ -86,44 +105,88 @@
             device_id=at(dp, dest), device_id_type=MESH,
         )
 
-    ahead = lax.rem(z + 1 + core * (nt - 2), nt)
-    hop = nt - 1 + 2 * core
-
-    def w_copy(step):
-        owner = lax.rem(z + (nt + hop) * step, nt)
-        return pltpu.make_async_remote_copy(
-            src_ref=w_t if step == 0 else w_all.at[owner],
-            dst_ref=w_all.at[owner],
-            send_sem=w_send.at[step], recv_sem=w_recv.at[step],
-            device_id=at(dp, ahead), device_id_type=MESH,
-        )
-
-    def w_across(step):
-        owner = lax.rem(z + (nt + hop) * step, nt)
-        return pltpu.make_async_remote_copy(
-            src_ref=w_all.at[owner], dst_ref=w_all.at[owner],
-            send_sem=pair_send.at[step], recv_sem=pair_recv.at[step],
+    grid = w_t.shape[1] // 384
+    many = grid * 3
+    deep = w_t.shape[0] // 3
+    mine = lax.rem(7 * column, columns)
+    owns = jnp.logical_and(mine < many, lax.rem(mine, 2) == core)
+
+    def spot(e):
+        return (
+            pl.ds(pl.multiple_of(lax.rem(e, 3) * deep, deep), deep),
+            pl.ds(pl.multiple_of((e // 3) * 384, 384), 384),
+        )
+
+    def w_copy(away):
+        lines, cols = spot(mine)
+        return pltpu.make_async_remote_copy(
+            src_ref=w_t.at[lines, cols], dst_ref=w_all.at[z, lines, cols],
+            send_sem=w_send.at[away], recv_sem=w_recv.at[away],
+            device_id=at(dp, lax.rem(z + away, nt)), device_id_type=MESH,
+        )
+
+    across_y = 4
+    across_x = columns // across_y
+    y = lax.rem(column, across_y)
+
+    def same_row(e):
+        return lax.rem(lax.rem(7 * e, columns), across_y) == y
+
+    def slab(e, by, along_x):
+        lines, cols = spot(e)
+        if along_x:
+            there = lax.rem(column + across_y * by, columns)
+            sem = slab_send.at[by]
+        else:
+            there = column - y + lax.rem(y + by, across_y)
+            sem = slab_send.at[across_x + e * across_y + by]
+        return pltpu.make_async_remote_copy(
+            src_ref=w_all.at[:, lines, cols], dst_ref=w_all.at[:, lines, cols],
+            send_sem=sem, recv_sem=slab_recv.at[e],
+            device_id=at(there * 2 + core, z), device_id_type=MESH,
+        )
+
+    def w_across(e):
+        lines, cols = spot(e)
+        return pltpu.make_async_remote_copy(
+            src_ref=w_all.at[:, lines, cols], dst_ref=w_all.at[:, lines, cols],
+            send_sem=pair_send.at[e], recv_sem=pair_recv.at[e],
             device_id=at(partner, z), device_id_type=MESH,
         )
 
-    half = nt // 2
-
-    def w_turn(step):
-        def turn():
-            if step > 0:
-                w_copy(step - 1).wait_recv()
-                w_across(step).start()
-            if step < half:
-                if step == half - 1:
-                    @pl.when(core == 0)
-                    def _():
-                        w_copy(step).start()
-                else:
-                    w_copy(step).start()
-        if step == half:
-            pl.when(core == 0)(turn)
-        else:
-            turn()
+    def w_hand():
+        @pl.when(owns)
+        def _():
+            @pl.loop(1, nt)
+            def _(away):
+                w_copy(away).wait_recv()
+
+            for by in range(1, across_x):
+                slab(mine, by, True).start()
+
+    def w_take(act):
+        @pl.loop(0, many)
+        def _(e):
+            @pl.when(lax.rem(e, 2) == core)
+            def _():
+                act(e)
+
+    def w_relay(e):
+        @pl.when(same_row(e))
+        def _():
+            @pl.when(e != mine)
+            def _():
+                slab(e, 1, True).wait_recv()
+
+            for by in range(1, across_y):
+                slab(e, by, False).start()
+            w_across(e).start()
+
+    def w_swap(e):
+        @pl.when(jnp.logical_not(same_row(e)))
+        def _():
+            slab(e, 1, False).wait_recv()
+            w_across(e).start()
 
     def partial(dest, cols):
         block = hid_i[:, pl.ds(pl.multiple_of(dest * rows, rows), rows)]
@@ -151,8 +214,20 @@
 
     for away in range(1, nt):
         hid_copy(away).start()
+
+    @pl.when(owns)
+    def _():
+        @pl.loop(1, nt)
+        def _(away):
+            w_copy(away).start()
+
     hid_all[z] = hid_t[:, pl.ds(pl.multiple_of(z * rows, rows), rows)]
-    w_all[z] = w_t[...]
+
+    @pl.when(owns)
+    def _():
+        lines, cols = spot(mine)
+        w_all[z, lines, cols] = w_t[lines, cols]
+
 
     for n, (kind, side, step) in enumerate(order):
         away = lengths[kind, side] - step
@@ -172,9 +247,10 @@
             else:
                 out_buf[n, :, local] = value.astype(BF)
         copy(n).start()
-        if n in (1, 5, 9, 12):
-            w_turn((1, 5, 9, 12).index(n))
-    w_turn(half)
+        if n == 1:
+            w_hand()
+        if n == 5:
+            w_take(w_relay)
 
     squares = jnp.zeros((rows, 1), F32)
     for kind in range(2):
@@ -206,12 +282,13 @@
 
     for away in range(1, nt):
         hid_copy(away).wait_recv()
-    for step in range(1, half):
-        w_across(step).wait_recv()
-
-    @pl.when(core == 1)
-    def _():
-        w_across(half).wait_recv()
+    w_take(w_swap)
+
+    @pl.loop(0, many)
+    def _(e):
+        @pl.when(lax.rem(e, 2) != core)
+        def _():
+            w_across(e).wait_recv()
 
     depth = hid_t.shape[0] * nt
     flat = hid_all[...].reshape(depth, rows)
@@ -232,25 +309,34 @@
         copy(n).wait_send()
     for away in range(1, nt):
         hid_copy(away).wait_send()
-    for step in range(half - 1):
-        w_copy(step).wait_send()
-    for step in range(1, half):
-        w_across(step).wait_send()
-
-    @pl.when(core == 0)
+    @pl.when(owns)
     def _():
-        w_copy(half - 1).wait_send()
-        w_across(half).wait_send()
-
-
-def head(nt, hid_i, w_i, pooled, hid_t, w_t, mrows):
+        @pl.loop(1, nt)
+        def _(away):
+            w_copy(away).wait_send()
+
+        for by in range(1, across_x):
+            slab(mine, by, True).wait_send()
+
+    def sent(e):
+        w_across(e).wait_send()
+
+        @pl.when(same_row(e))
+        def _():
+            for by in range(1, across_y):
+                slab(e, by, False).wait_send()
+
+    w_take(sent)
+
+
+def head(nt, columns, hid_i, w_i, pooled, hid_t, w_t, mrows):
     rows, width = pooled.shape
     items = len(chain_order(nt))
     most = CUTS[0][1]
     f = jax.ShapeDtypeStruct
     dma = pltpu.SemaphoreType.DMA
     return pl.pallas_call(
-        functools.partial(head_kernel, nt),
+        functools.partial(head_kernel, nt, columns),
         name="head",
         out_shape=(
             f((rows + EXTRA, width), BF),
@@ -260,7 +346,7 @@
             f((rows, width), F32),
             f((rows, 1), F32),
         ),
-        in_specs=[VM] * 6,
+        in_specs=[HB] * 5 + [VM],
         out_specs=(VM,) * 6,
         scratch_shapes=[
             pltpu.VMEM((items, rows, most), BF),
@@ -270,11 +356,17 @@
             pltpu.VMEM((rows, width), F32),
             pltpu.VMEM((nt, hid_t.shape[0], rows), BF),
             pltpu.VMEM((nt, hid_t.shape[0], width), BF),
+            pltpu.VMEM(hid_i.shape, BF),
+            pltpu.VMEM(w_i.shape, BF),
+            pltpu.VMEM(pooled.shape, BF),
+            pltpu.VMEM(hid_t.shape, BF),
+            pltpu.VMEM(w_t.shape, BF),
             dma((items,)), dma((items,)), dma((nt,)), dma((nt,)),
-            dma((nt,)), dma((nt,)), dma((nt,)), dma((nt,)),
+            dma((nt,)), dma((nt,)), dma((16,)), dma((16,)),
+            dma((64,)), dma((16,)), dma((5,)),
         ],
         compiler_params=pltpu.CompilerParams(
-            collective_id=0, has_side_effects=True, vmem_limit_bytes=48 << 20
+            collective_id=0, has_side_effects=True, vmem_limit_bytes=60 << 20
         ),
     )(hid_i, w_i, pooled, hid_t, w_t, mrows)
 
@@ -378,9 +470,6 @@
             across(0, 1).start()
     mine = pltpu.make_async_copy(txt, txts.at[2 * place(nt, 0)], local_sem)
     mine.start()
-    for (kind, side), length in lengths.items():
-        if length < nt // 2:
-            arrived(slots[kind, side, length - 1])
 
     for slot in range(2):
         image_copy(True, slot).wait()
@@ -405,26 +494,29 @@
             device_id=at(partner, z), device_id_type=MESH,
         )
 
-    far = nt // 2
-
-    @pl.loop(0, 2 * far)
-    def _(n):
-        piece(pair_send, pair_recv, n).wait_recv()
-
-    @pl.loop(2 * far + 2, 2 * nt)
-    def _(n):
-        piece(pair_send, pair_recv, n).wait_recv()
+    def taken(first, last):
+        @pl.loop(first, last)
+        def _(n):
+            piece(pair_send, pair_recv, n).wait_recv()
 
     @pl.loop(0, groups)
     def _(turn):
         g = groups - 1 - turn
 
-        @pl.when(turn == groups - 1)
+        @pl.when(turn == 1)
         def _():
-            arrived(slots[0, 0, far - 1])
-            arrived(slots[1, 1, far - 1])
-            for kind in range(2):
-                across(far, kind).wait_recv()
+            for (kind, side), length in lengths.items():
+                if length < groups:
+                    arrived(slots[kind, side, length - 1])
+
+        @pl.when(turn == 2)
+        def _():
+            for (kind, side), length in lengths.items():
+                if length == groups:
+                    arrived(slots[kind, side, length - 1])
+
+        taken(2 * turn, 2 * turn + 2)
+        taken(2 * (nt - 1 - turn), 2 * (nt - turn))
 
         @pl.loop(0, 2)
         def _(h):
@@ -611,7 +703,7 @@
         line == 0, match[None, :] >> 8, jnp.where(line == 1, match[None, :] & 255, 0)
     ).astype(BF)
     img_ext, img_unit, img_len, txt_low, txt_unit, txt_len = head(
-        nt, img_hidden.T, img_down, img_pooled, txt_hidden.T, txt_proj, mrows
+        nt, columns, img_hidden.T, img_down, img_pooled, txt_hidden.T, txt_proj, mrows
     )
     img_back, text_dunit = lax.switch(
         window,

time: 144 us -> 129 us (0.90)
  Pallas kernels: 131 us -> 119 us
  local copies, waits for them, and re-layouts: 5.44 us -> 0.98 us
  other arithmetic: 3.84 us -> 6.09 us
    pallas_call x1, Pallas kernels: 68.9 us -> 61.2 us  [window_pass(): pl.pallas_call(functools.partial(window_kernel, nt, columns, window), nam...]
    unnamed x10 -> x4, local copies, waits for them, and re-layouts: 5.44 us -> 0.98 us
    pallas_call x1, Pallas kernels: 62.4 us -> 58 us  [head(): pl.pallas_call(functools.partial(head_kernel, nt, columns), name='head',...]
    pallas_call x2, other arithmetic: 0.22 us -> 1.89 us  [head(): pl.pallas_call(functools.partial(head_kernel, nt, columns), name='head',...]
where the time goes in v3:
time: 129 us; the launch traced here: 128 us
  Pallas kernels  119 us (92%)
  other arithmetic  6.09 us (5%)
  between operations  1.33 us (1%)
    pallas_call x1, Pallas kernels, window_pass(): pl.pallas_call(functools.partial(window_kernel, nt, columns, window), nam...  61.2 us
    pallas_call x1, Pallas kernels, head(): pl.pallas_call(functools.partial(head_kernel, nt, columns), name='head',...  58 us

profile of v3, /device:TPU:1, one launch (start us, length us, event | category | flops | bytes accessed | tf_op | source)
XLA Modules:
  0.0 128.4 jit_solution(2386813946800290999)
XLA Ops:
  1.3 0.7 broadcast_shift-right-arithmetic_fusion
  1.9 0.7 select_convert_fusion.mrows
  2.6 58.0 %head.1 = (bf16[144,1152]{1,0:T(8,128)(2,1)S(1)}, f32[128,1152]{1,0:T(8,128)}, f32[128,1]{1,0:T(8,128)}, bf16[128,1152]{1,0:T(8,128)(2,1)S(1)}, f32[128,1152]{1,0:T(8,128)}, /*index=5*/f32[128,1]{1,0:T(8,128)}) custom-call(bf16[538,1024]{1,0:T(8,128)(2,1)} %bitcast.9, bf16[538,1152]{1,0:T(8,128)(2,1)} %w_i_hbm.1, bf16[128,1152]{1,0:T(8,128)(2,1)} %pooled_hbm.1, ...), custom_call_target="tpu_custom_call" | custom-call | tf_op jit(solution)/shard_map/head/pallas_call | solution.py:338
  60.6 0.9 reduce
  61.6 1.0 reduce.1
  62.5 0.0 copy-start
  62.5 62.0 %conditional.1 = ((bf16[2,144,1152]{2,1,0:T(8,128)(2,1)S(1)}, f32[128,1152]{1,0:T(8,128)S(1)})) conditional(s32[]{:T(128)} %bitcast, (f32[1]{0:T(128)}, f32[1]{0:T(128)}, bf16[144,1152]{1,0:T(8,128)(2,1)S(1)}, bf16[128,1152]{1,0:T(8,128)(2,1)S(1)}) %tuple.56, (f32[1]{0:T(128)}, f32[1]{0:T(128)}, ...), branch_computations={%region_0.1_spmd, %region_1.2_spmd, %region_2.3_spmd, %region_3.4_... | conditional | bytes 8 | solution.py:708
  62.6 61.2 %window_2.1 = (bf16[2,144,1152]{2,1,0:T(8,128)(2,1)S(1)}, f32[128,1152]{1,0:T(8,128)S(1)}) custom-call(f32[1]{0:T(128)} %get-tuple-element.136.log_temp, f32[1]{0:T(128)} %get-tuple-element.137.bias, bf16[144,1152]{1,0:T(8,128)(2,1)S(1)} %get-tuple-element.138.img, bf16[128,1152]{1,0:T(8,128)(2,1)S(1)} %get-tuple-element.139.txt), custom_call_target="tpu_custom_call" | custom-call | tf_op jit(solution)/shard_map/cond/branch_2_fun/window_2/pallas_call | solution.py:662
  124.5 0.0 copy-done
  124.5 0.1 multiply_reduce_fusion
  124.7 1.0 subtract_divide_fusion
  125.6 0.0 copy-start.1
  125.6 0.1 convert_element_type.7
  125.7 1.0 copy-done.1
  126.7 0.2 multiply_reduce_fusion.1
  126.9 1.0 subtract_divide_fusion.1
  127.8 0.5 slice_reduce_fusion
  (1 shorter events, 0.0 us)
Async XLA Ops:
  62.5 62.0 %copy-start = (f32[128,1152]{1,0:T(8,128)S(1)}, f32[128,1152]{1,0:T(8,128)}, u32[]{:S(2)}) copy-start(f32[128,1152]{1,0:T(8,128)} %get-tuple-element.209) | copy-start | bytes 1769476
  125.6 1.1 copy-start.1

commit v4 on v3

--- a/solution.py
+++ b/solution.py
@@ -212,9 +212,6 @@
             device_id=at(dp, right if side == 0 else left), device_id_type=MESH,
         )
 
-    for away in range(1, nt):
-        hid_copy(away).start()
-
     @pl.when(owns)
     def _():
         @pl.loop(1, nt)
@@ -247,10 +244,48 @@
             else:
                 out_buf[n, :, local] = value.astype(BF)
         copy(n).start()
-        if n == 1:
+        if n == 3:
+            for distance in range(1, nt):
+                hid_copy(distance).start()
             w_hand()
         if n == 5:
             w_take(w_relay)
+
+    def finish(squares, unit_ref, len_ref, low_ref):
+        length = jnp.sqrt(squares + 1e-06)
+        len_ref[...] = jnp.broadcast_to(length, len_ref.shape)
+
+        @pl.loop(0, width // 128)
+        def _(t):
+            cols = pl.ds(pl.multiple_of(t * 128, 128), 128)
+            unit = acc[:, cols] / length
+            unit_ref[:, cols] = unit
+            low_ref[pl.ds(0, rows), cols] = unit.astype(BF)
+
+    for away in range(1, nt):
+        hid_copy(away).wait_recv()
+    w_take(w_swap)
+
+    @pl.loop(0, many)
+    def _(e):
+        @pl.when(lax.rem(e, 2) != core)
+        def _():
+            w_across(e).wait_recv()
+
+    depth = hid_t.shape[0] * nt
+    flat = hid_all[...].reshape(depth, rows)
+
+    def txt_tile(t, squares):
+        cols = pl.ds(pl.multiple_of(t * 384, 384), 384)
+        value = lax.dot_general(
+            flat, w_all[:, :, cols].reshape(depth, 384), (((0,), (0,)), ((), ())),
+            preferred_element_type=F32,
+        )
+        acc[:, cols] = value
+        return squares + jnp.sum(value * value, axis=1, keepdims=True)
+
+    squares = lax.fori_loop(0, width // 384, txt_tile, jnp.zeros((rows, 1), F32))
+    finish(squares, txt_unit, txt_len, txt_low)
 
     squares = jnp.zeros((rows, 1), F32)
     for kind in range(2):
@@ -265,45 +300,9 @@
             acc[:, cols] = value
             squares = squares + jnp.sum(value * value, axis=1, keepdims=True)
 
-    def finish(squares, unit_ref, len_ref, low_ref):
-        length = jnp.sqrt(squares + 1e-06)
-        len_ref[...] = length
-
-        @pl.loop(0, width // 128)
-        def _(t):
-            cols = pl.ds(pl.multiple_of(t * 128, 128), 128)
-            unit = acc[:, cols] / length
-            unit_ref[:, cols] = unit
-            low_ref[pl.ds(0, rows), cols] = unit.astype(BF)
-
     finish(squares, img_unit, img_len, img_ext)
     img_ext[pl.ds(rows, EXTRA), :] = jnp.zeros((EXTRA, width), BF)
     img_ext[pl.ds(rows, EXTRA), pl.ds(0, rows)] = mrows[...]
-
-    for away in range(1, nt):
-        hid_copy(away).wait_recv()
-    w_take(w_swap)
-
-    @pl.loop(0, many)
-    def _(e):
-        @pl.when(lax.rem(e, 2) != core)
-        def _():
-            w_across(e).wait_recv()
-
-    depth = hid_t.shape[0] * nt
-    flat = hid_all[...].reshape(depth, rows)
-
-    def txt_tile(t, squares):
-        cols = pl.ds(pl.multiple_of(t * 384, 384), 384)
-        value = lax.dot_general(
-            flat, w_all[:, :, cols].reshape(depth, 384), (((0,), (0,)), ((), ())),
-            preferred_element_type=F32,
-        )
-        acc[:, cols] = value
-        return squares + jnp.sum(value * value, axis=1, keepdims=True)
-
-    squares = lax.fori_loop(0, width // 384, txt_tile, jnp.zeros((rows, 1), F32))
-    finish(squares, txt_unit, txt_len, txt_low)
 
     for n in range(len(order)):
         copy(n).wait_send()
@@ -341,10 +340,10 @@
         out_shape=(
             f((rows + EXTRA, width), BF),
             f((rows, width), F32),
-            f((rows, 1), F32),
+            f((rows, 128), F32),
             f((rows, width), BF),
             f((rows, width), F32),
-            f((rows, 1), F32),
+            f((rows, 128), F32),
         ),
         in_specs=[HB] * 5 + [VM],
         out_specs=(VM,) * 6,
@@ -715,10 +714,10 @@
     row_loss = jnp.sum(back[:, rows:rows + 2, :rows], axis=(0, 1))
     img_grad = (
         image_dunit - img_unit * jnp.sum(img_unit * image_dunit, axis=1, keepdims=True)
-    ) / img_len
+    ) / img_len[:, :1]
     txt_grad = (
         text_dunit - txt_unit * jnp.sum(txt_unit * text_dunit, axis=1, keepdims=True)
-    ) / txt_len
+    ) / txt_len[:, :1]
     return (img_grad, txt_grad, row_loss)
 
 

time: 129 us -> 126 us (0.977)
  Pallas kernels: 119 us -> 116 us
  other arithmetic: 6.09 us -> 4.19 us
  local copies, waits for them, and re-layouts: 0.98 us -> 2.87 us
    pallas_call x1, Pallas kernels: 58 us -> 51.3 us  [head(): pl.pallas_call(functools.partial(head_kernel, nt, columns), name='head',...]
    pallas_call x1, Pallas kernels: 61.2 us -> 64.8 us  [window_pass(): pl.pallas_call(functools.partial(window_kernel, nt, columns, window), nam...]
    pallas_call x2 -> x0, other arithmetic: 1.89 us -> none  [head(): pl.pallas_call(functools.partial(head_kernel, nt, columns), name='head',...]
    slice x0 -> x2, local copies, waits for them, and re-layouts: none -> 1.89 us  [the longest x1 0.95 us: body(): txt_len[:, :1]]
where the time goes in v4:
time: 126 us; the launch traced here: 125 us
  Pallas kernels  116 us (92%)
  other arithmetic  4.19 us (3%)
  local copies, waits for them, and re-layouts  2.87 us (2%)
  between operations  1.33 us (1%)
    pallas_call x1, Pallas kernels, window_pass(): pl.pallas_call(functools.partial(window_kernel, nt, columns, window), nam...  64.8 us
    pallas_call x1, Pallas kernels, head(): pl.pallas_call(functools.partial(head_kernel, nt, columns), name='head',...  51.3 us

profile of v4, /device:TPU:1, one launch (start us, length us, event | category | flops | bytes accessed | tf_op | source)
XLA Modules:
  0.0 125.3 jit_solution(7167791492002002774)
XLA Ops:
  1.3 0.7 broadcast_shift-right-arithmetic_fusion
  1.9 0.7 select_convert_fusion.mrows
  2.6 51.3 %head.1 = (bf16[144,1152]{1,0:T(8,128)(2,1)S(1)}, f32[128,1152]{1,0:T(8,128)}, f32[128,128]{1,0:T(8,128)}, bf16[128,1152]{1,0:T(8,128)(2,1)S(1)}, f32[128,1152]{1,0:T(8,128)}, /*index=5*/f32[128,128]{1,0:T(8,128)}) custom-call(bf16[538,1024]{1,0:T(8,128)(2,1)} %bitcast.9, bf16[538,1152]{1,0:T(8,128)(2,1)} %w_i_hbm.1, bf16[128,1152]{1,0:T(8,128)(2,1)} %pooled_hbm.1, ...), custom_call_target="tpu_custom_call" | custom-call | tf_op jit(solution)/shard_map/head/pallas_call | solution.py:337
  54.0 0.9 slice_reduce_fusion.1
  54.9 1.0 slice_reduce_fusion
  55.9 0.0 copy-start
  55.9 65.5 %conditional.1 = ((bf16[2,144,1152]{2,1,0:T(8,128)(2,1)S(1)}, f32[128,1152]{1,0:T(8,128)S(1)})) conditional(s32[]{:T(128)} %bitcast, (f32[1]{0:T(128)}, f32[1]{0:T(128)}, bf16[144,1152]{1,0:T(8,128)(2,1)S(1)}, bf16[128,1152]{1,0:T(8,128)(2,1)S(1)}) %tuple.56, (f32[1]{0:T(128)}, f32[1]{0:T(128)}, ...), branch_computations={%region_0.1_spmd, %region_1.2_spmd, %region_2.3_spmd, %region_3.4_... | conditional | bytes 8 | solution.py:707
  55.9 64.8 %window_3.1 = (bf16[2,144,1152]{2,1,0:T(8,128)(2,1)S(1)}, f32[128,1152]{1,0:T(8,128)S(1)}) custom-call(f32[1]{0:T(128)} %get-tuple-element.140.log_temp, f32[1]{0:T(128)} %get-tuple-element.141.bias, bf16[144,1152]{1,0:T(8,128)(2,1)S(1)} %get-tuple-element.142.img, bf16[128,1152]{1,0:T(8,128)(2,1)S(1)} %get-tuple-element.143.txt), custom_call_target="tpu_custom_call" | custom-call | tf_op jit(solution)/shard_map/cond/branch_3_fun/window_3/pallas_call | solution.py:661
  121.4 0.0 copy-done
  121.4 0.1 multiply_reduce_fusion
  121.5 1.0 subtract_divide_fusion
  122.5 0.0 copy-start.1
  122.5 0.1 convert_element_type.7
  122.6 1.0 copy-done.1
  123.6 0.2 multiply_reduce_fusion.1
  123.7 1.0 subtract_divide_fusion.1
  124.7 0.5 slice_reduce_fusion.2
  (1 shorter events, 0.0 us)
Async XLA Ops:
  55.9 65.5 %copy-start = (f32[128,1152]{1,0:T(8,128)S(1)}, f32[128,1152]{1,0:T(8,128)}, u32[]{:S(2)}) copy-start(f32[128,1152]{1,0:T(8,128)} %get-tuple-element.209) | copy-start | bytes 1769476
  122.5 1.1 copy-start.1

commit v5 on v4

--- a/solution.py
+++ b/solution.py
@@ -340,10 +340,10 @@
         out_shape=(
             f((rows + EXTRA, width), BF),
             f((rows, width), F32),
-            f((rows, 128), F32),
+            f((rows, width), F32),
             f((rows, width), BF),
             f((rows, width), F32),
-            f((rows, 128), F32),
+            f((rows, width), F32),
         ),
         in_specs=[HB] * 5 + [VM],
         out_specs=(VM,) * 6,
@@ -714,10 +714,10 @@
     row_loss = jnp.sum(back[:, rows:rows + 2, :rows], axis=(0, 1))
     img_grad = (
         image_dunit - img_unit * jnp.sum(img_unit * image_dunit, axis=1, keepdims=True)
-    ) / img_len[:, :1]
+    ) / img_len
     txt_grad = (
         text_dunit - txt_unit * jnp.sum(txt_unit * text_dunit, axis=1, keepdims=True)
-    ) / txt_len[:, :1]
+    ) / txt_len
     return (img_grad, txt_grad, row_loss)
 
 

time: 126 us -> 128 us (1.016)
  Pallas kernels: 116 us -> 118 us
    slice x2 -> x0, local copies, waits for them, and re-layouts: 1.89 us -> none  [the longest x1 0.95 us: body(): txt_len[:, :1]]
    unnamed x4 -> x8, local copies, waits for them, and re-layouts: 0.98 us -> 2.79 us
    pallas_call x1, Pallas kernels: 64.8 us -> 66.1 us  [window_pass(): pl.pallas_call(functools.partial(window_kernel, nt, columns, window), nam...]
where the time goes in v5:
time: 128 us; the launch traced here: 127 us
  Pallas kernels  118 us (92%)
  other arithmetic  4.2 us (3%)
  local copies, waits for them, and re-layouts  2.79 us (2%)
  between operations  1.33 us (1%)
    pallas_call x1, Pallas kernels, window_pass(): pl.pallas_call(functools.partial(window_kernel, nt, columns, window), nam...  66.1 us
    pallas_call x1, Pallas kernels, head(): pl.pallas_call(functools.partial(head_kernel, nt, columns), name='head',...  51.7 us
    unnamed x8, local copies, waits for them, and re-layouts  2.79 us

profile of v5, /device:TPU:1, one launch (start us, length us, event | category | flops | bytes accessed | tf_op | source)
XLA Modules:
  0.0 127.0 jit_solution(7385317046295851788)
XLA Ops:
  1.3 0.7 broadcast_shift-right-arithmetic_fusion
  1.9 0.7 select_convert_fusion.mrows
  2.6 51.7 %head.1 = (bf16[144,1152]{1,0:T(8,128)(2,1)S(1)}, f32[128,1152]{1,0:T(8,128)}, f32[128,1152]{1,0:T(8,128)}, bf16[128,1152]{1,0:T(8,128)(2,1)S(1)}, f32[128,1152]{1,0:T(8,128)}, /*index=5*/f32[128,1152]{1,0:T(8,128)}) custom-call(bf16[538,1024]{1,0:T(8,128)(2,1)} %bitcast.9, bf16[538,1152]{1,0:T(8,128)(2,1)} %w_i_hbm.1, bf16[128,1152]{1,0:T(8,128)(2,1)} %pooled_hbm.1, ...), custom_call_target="tpu_custom_call" | custom-call | tf_op jit(solution)/shard_map/head/pallas_call | solution.py:337
  54.3 0.0 copy-start
  54.3 67.0 %conditional.1 = ((bf16[2,144,1152]{2,1,0:T(8,128)(2,1)S(1)}, f32[128,1152]{1,0:T(8,128)S(1)})) conditional(s32[]{:T(128)} %bitcast, (f32[1]{0:T(128)}, f32[1]{0:T(128)}, bf16[144,1152]{1,0:T(8,128)(2,1)S(1)}, bf16[128,1152]{1,0:T(8,128)(2,1)S(1)}) %tuple.56, (f32[1]{0:T(128)}, f32[1]{0:T(128)}, ...), branch_computations={%region_0.1_spmd, %region_1.2_spmd, %region_2.3_spmd, %region_3.4_... | conditional | bytes 8 | solution.py:707
  54.9 66.1 %window_14.1 = (bf16[2,144,1152]{2,1,0:T(8,128)(2,1)S(1)}, f32[128,1152]{1,0:T(8,128)S(1)}) custom-call(f32[1]{0:T(128)} %get-tuple-element.184.log_temp, f32[1]{0:T(128)} %get-tuple-element.185.bias, bf16[144,1152]{1,0:T(8,128)(2,1)S(1)} %get-tuple-element.186.img, bf16[128,1152]{1,0:T(8,128)(2,1)S(1)} %get-tuple-element.187.txt), custom_call_target="tpu_custom_call" | custom-call | tf_op jit(solution)/shard_map/cond/branch_14_fun/window_14/pallas_call | solution.py:661
  121.3 0.0 copy-start.2
  121.3 0.0 copy-done
  121.3 0.1 multiply_reduce_fusion
  121.5 0.9 copy-done.2
  122.4 1.0 subtract_divide_fusion
  123.4 0.0 copy-start.1
  123.4 0.1 convert_element_type.7
  123.5 1.0 copy-done.1
  124.4 0.0 copy-start.3
  124.4 0.2 multiply_reduce_fusion.1
  124.6 0.9 copy-done.3
  125.5 1.0 subtract_divide_fusion.1
  126.5 0.5 slice_reduce_fusion
  (1 shorter events, 0.0 us)
Async XLA Ops:
  54.3 67.0 %copy-start = (f32[128,1152]{1,0:T(8,128)S(1)}, f32[128,1152]{1,0:T(8,128)}, u32[]{:S(2)}) copy-start(f32[128,1152]{1,0:T(8,128)} %get-tuple-element.209) | copy-start | bytes 1769476
  121.3 1.1 copy-start.2
  123.4 1.1 copy-start.1
  124.4 1.1 copy-start.3
